TPU v7x, 256 devices: a whole 4x4x8 slice. The times are simulated.
256 devices in a mesh: ctx: 64 (over z, x_hi, y), tp: 4 (over x_lo, core).
Axes of the slice: x: 4 (x_hi: 2, x_lo: 2; x = x_hi * 2 + x_lo), y: 4, z: 8, core: 2. Of those that a mesh axis runs over, the one named last changes fastest.
Arguments:
- queries: bfloat16 [32768, 4096], P('ctx', 'tp'), may hold values from -22 to 22
- keys: bfloat16 [32768, 512], P('ctx', 'tp'), may hold values from -22 to 22
- values: bfloat16 [32768, 512], P('ctx', 'tp'), may hold values from -36 to 36
- positions: int32 [3, 32768], P(None, 'ctx'), may hold values from 0 to 32767
- segment_ids: int32 [32768], replicated, may hold values from 0 to 31, never falling along the last dimension, each value on 1 to 2048 neighbouring positions
- out_weight: bfloat16 [4096, 8192], P('tp', 'ctx'), may hold values from -0.09375 to 0.09375
- residual: bfloat16 [32768, 8192], P(('ctx', 'tp')), may hold values from -3 to 3
Outputs:
- layer_out: bfloat16 [32768, 8192], P(('ctx', 'tp'))
Inputs may be any that keep to these rules, and one draw needn't show every extreme that they name: `segment_ids`: ids never fall along the sequence; each document has 1 to 2048 tokens, and one has exactly 2048.
All inputs are finite; a program needn't handle non-finite values.
Results may differ from a plain program's by a relative error of at most 0.013.
Values may be sent and summed in bfloat16 or wider, within the bound.
A program may use at most 128 MiB of HBM per device.

v0:
```python
import math

import jax
import jax.numpy as jnp
from jax import lax
from jax.sharding import PartitionSpec as P

HD = 128
DOC = 2048


theta_base = 1000000.0


def from_behind(block, axis, distance):
    devices = range(lax.axis_size(axis))
    route = [(i - distance, i) for i in devices if i - distance in devices]
    return lax.ppermute(block, axis, route)


def rotary_tables(positions):
    half_dim = HD // 2
    freq_index = jnp.arange(half_dim)
    inv_freq = theta_base ** (-2.0 * freq_index.astype(jnp.float32) / HD)
    first_end = HD // 8
    second_end = first_end + 3 * HD // 16
    place = positions.astype(jnp.float32)
    chosen = jnp.where(
        freq_index[None, :] < first_end,
        place[0][:, None],
        jnp.where(freq_index[None, :] < second_end, place[1][:, None], place[2][:, None]),
    )
    angle = chosen * inv_freq[None, :]
    return (jnp.cos(angle), jnp.sin(angle))


def rotate(vectors, cosine_table, sine_table):
    half_dim = HD // 2
    lower_half = vectors[..., :half_dim]
    upper_half = vectors[..., half_dim:]
    cos_b = cosine_table[:, None, :]
    sin_b = sine_table[:, None, :]
    return jnp.concatenate(
        [lower_half * cos_b - upper_half * sin_b, upper_half * cos_b + lower_half * sin_b], axis=-1
    )


def on_device(queries, keys, values, positions, segment_ids, out_weight, residual):
    tok_rows = queries.shape[0]
    local_heads = queries.shape[1] // HD
    local_kv = keys.shape[1] // HD
    group_size = local_heads // local_kv
    reach_blocks = (DOC + tok_rows - 2) // tok_rows
    my_start = lax.axis_index("ctx") * tok_rows
    cosine_table, sine_table = rotary_tables(positions)
    rot_q = rotate(
        queries.reshape(tok_rows, local_heads, HD).astype(jnp.float32), cosine_table, sine_table
    ).astype(jnp.bfloat16)
    grouped = rot_q.reshape(tok_rows, local_kv, group_size, HD).transpose(1, 2, 0, 3)
    rot_k = rotate(
        keys.reshape(tok_rows, local_kv, HD).astype(jnp.float32), cosine_table, sine_table
    ).astype(jnp.bfloat16)
    key_flat = rot_k.reshape(tok_rows, local_kv * HD)
    query_index = my_start + jnp.arange(tok_rows, dtype=jnp.int32)
    query_seg = lax.dynamic_slice_in_dim(segment_ids, my_start, tok_rows, 0)
    score_scale = 1.0 / math.sqrt(HD)
    block_rows = math.gcd(tok_rows, 512)
    block_count = tok_rows // block_rows

    def absorb(running, stacked, offset):
        key_blocks = stacked[0].reshape(block_count, block_rows, local_kv, HD)
        value_blocks = stacked[1].reshape(block_count, block_rows, local_kv, HD)

        def advance(block_index, carried):
            key_block = lax.dynamic_index_in_dim(key_blocks, block_index, 0, keepdims=False)
            value_block = lax.dynamic_index_in_dim(value_blocks, block_index, 0, keepdims=False)
            key_first = offset + block_index * block_rows
            key_index = key_first + jnp.arange(block_rows, dtype=jnp.int32)
            key_seg = lax.dynamic_slice_in_dim(
                segment_ids, jnp.maximum(key_first, 0), block_rows, 0
            )
            allowed = (
                (key_index[None, :] <= query_index[:, None])
                & (key_index[None, :] >= 0)
                & (key_seg[None, :] == query_seg[:, None])
            )

            def update(current):
                row_peak, row_sum, weighted = current
                score = (
                    jnp.einsum(
                        "kgtd,nkd->kgtn", grouped, key_block, preferred_element_type=jnp.float32
                    )
                    * score_scale
                )
                score = jnp.where(allowed, score, -1e30)
                new_peak = jnp.maximum(row_peak, jnp.max(score, axis=-1))
                prob = jnp.where(allowed, jnp.exp(score - new_peak[..., None]), 0.0)
                rescale = jnp.exp(row_peak - new_peak)
                row_sum = row_sum * rescale + jnp.sum(prob, axis=-1)
                weighted = weighted * rescale[..., None] + jnp.einsum(
                    "kgtn,nkd->kgtd",
                    prob.astype(jnp.bfloat16),
                    value_block,
                    preferred_element_type=jnp.float32,
                )
                return (new_peak, row_sum, weighted)

            def keep_state(current):
                return current

            return lax.cond(jnp.any(allowed), update, keep_state, carried)

        return lax.fori_loop(0, block_count, advance, running)

    initial = (
        jnp.full((local_kv, group_size, tok_rows), -1e30, jnp.float32),
        jnp.zeros((local_kv, group_size, tok_rows), jnp.float32),
        jnp.zeros((local_kv, group_size, tok_rows, HD), jnp.float32),
    )
    own_pair = jnp.stack([key_flat, values], axis=0)
    state = absorb(initial, own_pair, my_start)

    def next_block(step_index, carried):
        moving, running = carried
        moving = from_behind(moving, "ctx", 1)
        running = absorb(running, moving, my_start - step_index * tok_rows)
        return (moving, running)

    moving, state = lax.fori_loop(1, reach_blocks + 1, next_block, (own_pair, state))
    row_peak, row_sum, weighted = state
    attended = (
        (weighted / row_sum[..., None])
        .transpose(2, 0, 1, 3)
        .reshape(tok_rows, local_heads * HD)
        .astype(jnp.bfloat16)
    )
    partial_sum = jnp.dot(
        attended,
        lax.all_gather(out_weight, "ctx", axis=1, tiled=True),
        preferred_element_type=jnp.float32,
    )
    partial_sum = partial_sum.astype(jnp.bfloat16).astype(jnp.float32)
    shared = lax.psum_scatter(
        partial_sum.astype(jnp.bfloat16), "tp", scatter_dimension=0, tiled=True
    ).astype(jnp.float32)
    return (shared + residual.astype(jnp.float32)).astype(jnp.bfloat16)


def solution(mesh):
    return jax.shard_map(
        on_device,
        mesh=mesh,
        in_specs=(
            P("ctx", "tp"),
            P("ctx", "tp"),
            P("ctx", "tp"),
            P(None, "ctx"),
            P(),
            P("tp", "ctx"),
            P(("ctx", "tp"), None),
        ),
        out_specs=P(("ctx", "tp"), None),
        check_vma=False,
    )
```

profile of v0, /device:TPU:15, one launch (start us, length us, event | category | flops | bytes accessed | tf_op | source)
XLA Modules:
  0.0 394.6 jit_solution(13520080402836505690)
XLA Ops:
  8.0 1.5 copy.12
  10.7 1.0 fusion.43
  14.2 1.5 broadcast_in_dim.135
  15.7 2.2 subtract_convert_fusion.1
  18.0 8.1 %conditional.2 = ((f32[1,8,512]{2,1,0:T(8,128)S(1)}, f32[1,8,512]{2,1,0:T(8,128)S(1)}, f32[1,8,512,128]{3,2,1,0:T(8,128)})) conditional(s32[]{:T(128)} %convert_element_type.95, (f32[1,8,512]{2,1,0:T(8,128)S(1)}, f32[1,8,512]{2,1,0:T(8,128)S(1)}, f32[1,8,512,128]{3,2,1,0:T(8,128)}) %tuple.39, (pred[512,512]{0,1:T(8,128)(4,1)S(1)}, ...), branch_computations={%region_1.2_spmd, %region_2.0_spmd} | conditional | flops 1102065664 | bytes 49021044 | solution.py:112
  18.0 1.5 fusion.2
  19.6 2.0 fusion.4
  21.6 3.1 bitcast_add_fusion
  24.8 1.3 copy-done.1
  26.1 1.0 pad_maximum_fusion
  27.2 57.0 %while.28 = (s32[]{:T(128)}, bf16[2,512,128]{2,1,0:T(8,128)(2,1)S(1)}, f32[1,8,512]{2,1,0:T(8,128)S(1)}, f32[1,8,512]{2,1,0:T(8,128)S(1)}, f32[1,8,512,128]{3,2,...) while((s32[]{:T(128)}, ...), condition=%wide.region_11.12_spmd.clone.clone, body=%wide.region_5.11_spmd.clone.clone.sunk | while | flops 1103378432 | bytes 50349432 | solution.py:130
  27.2 3.2 collective-permute-start
  31.2 1.1 fusion.49
  33.0 4.7 %collective-permute-done = bf16[2,512,128]{2,1,0:T(8,128)(2,1)S(1)} collective-permute-done((bf16[2,512,128]{2,1,0:T(8,128)(2,1)S(1)}, bf16[2,512,128]{2,1,0:T(8,128)(2,1)S(1)}, u32[]{:S(2)}, u32[]{:S(2)}) %collective-permute-start) | collective-permute-done | bytes 262176 | tf_op jit(solution)/shard_map/while/body/eval_jaxpr/ppermute | solution.py:18
  37.7 6.8 %conditional.6 = ((f32[1,8,512]{2,1,0:T(8,128)S(1)}, f32[1,8,512]{2,1,0:T(8,128)S(1)}, f32[1,8,512,128]{3,2,1,0:T(8,128)})) conditional(s32[]{:T(128)} %convert_element_type.124, (f32[1,8,512]{2,1,0:T(8,128)S(1)}, f32[1,8,512]{2,1,0:T(8,128)S(1)}, f32[1,8,512,128]{3,2,1,0:T(8,128)}) %tuple.80, (pred[512,512]{0,1:T(8,128)(4,1)S(1)}, ...), branch_computations={%region_7.7_spmd, %region_8.10_spmd} | conditional | flops 1102065664 | bytes 48496728 | solution.py:112
  37.7 1.5 fusion.18
  39.2 3.1 bitcast_add_fusion.2
  42.4 2.0 fusion.20
  44.5 3.2 collective-permute-start
  48.6 1.1 fusion.49
  50.4 3.5 collective-permute-done
  53.9 1.9 collective-permute-start
  56.6 1.1 fusion.49
  58.4 11.1 %collective-permute-done = bf16[2,512,128]{2,1,0:T(8,128)(2,1)S(1)} collective-permute-done((bf16[2,512,128]{2,1,0:T(8,128)(2,1)S(1)}, bf16[2,512,128]{2,1,0:T(8,128)(2,1)S(1)}, u32[]{:S(2)}, u32[]{:S(2)}) %collective-permute-start) | collective-permute-done | bytes 262176 | tf_op jit(solution)/shard_map/while/body/eval_jaxpr/ppermute | solution.py:18
  69.5 7.0 %collective-permute-start = (bf16[2,512,128]{2,1,0:T(8,128)(2,1)S(1)}, bf16[2,512,128]{2,1,0:T(8,128)(2,1)S(1)}, u32[]{:S(2)}, u32[]{:S(2)}) collective-permute-start(bf16[2,512,128]{2,1,0:T(8,128)(2,1)S(1)} %get-tuple-element.546), channel_id=1, source_target_pairs={{0,4},{4,8},{8,12},{12,16},{16,20},{20,24},{24,28},{28,32},{32,36}... | collective-permute-start | bytes 786440 | tf_op jit(solution)/shard_map/while/body/eval_jaxpr/ppermute | solution.py:18
  77.3 1.1 fusion.49
  79.1 5.0 %collective-permute-done = bf16[2,512,128]{2,1,0:T(8,128)(2,1)S(1)} collective-permute-done((bf16[2,512,128]{2,1,0:T(8,128)(2,1)S(1)}, bf16[2,512,128]{2,1,0:T(8,128)(2,1)S(1)}, u32[]{:S(2)}, u32[]{:S(2)}) %collective-permute-start) | collective-permute-done | bytes 262176 | tf_op jit(solution)/shard_map/while/body/eval_jaxpr/ppermute | solution.py:18
  84.2 1.9 copy.15
  86.4 198.6 %all-gather.2.cloned.1.call-done = bf16[1024,8192]{1,0:T(8,128)(2,1)} async-done(((bf16[1024,128]{1,0:T(8,128)(2,1)}), bf16[1024,8192]{1,0:T(8,128)(2,1)}) %all-gather.2.cloned.1.call-update) | async-done | bytes 16777232 | tf_op jit(solution)/shard_map/all_gather | solution.py:140
  285.1 16.9 %convolution_convert_fusion = bf16[512,8192]{1,0:T(8,128)(2,1)} fusion(bf16[512,1024]{0,1:T(8,128)(2,1)S(1)} %bitcast.79, bf16[1024,8192]{1,0:T(8,128)(2,1)} %all-gather.2.cloned.1.call-done), kind=kOutput, calls=%fused_computation.45 | convolution fusion | flops 8594128896 | bytes 26214400 | tf_op jit(solution)/shard_map/dot_general | solution.py:138
  302.1 82.2 %reduce-scatter.2.cloned.1.call-done = bf16[128,8192]{1,0:T(8,128)(2,1)} async-done(((bf16[512,8192]{1,0:T(8,128)(2,1)}), bf16[128,8192]{1,0:T(8,128)(2,1)}) %reduce-scatter.2.cloned.1.call-update) | async-done | bytes 2097168 | tf_op jit(solution)/shard_map/reduce_scatter | solution.py:144
  384.3 3.4 add_convert_fusion
  (78 shorter events, 8.1 us)
Async XLA Ops:
  6.5 9.1 %copy-start.5 = (bf16[512,128]{1,0:T(8,128)(2,1)S(1)}, bf16[512,128]{1,0:T(8,128)(2,1)}, u32[]{:S(2)}) copy-start(bf16[512,128]{1,0:T(8,128)(2,1)} %param.14) | copy-start | bytes 393220
  6.5 278.5 %all-gather.2.cloned.1.call-start = ((), (), s32[]{:S(2)}) async-start(), calls=%async_computation.1 | async-start | bytes 17039360 | tf_op jit(solution)/shard_map/all_gather | solution.py:140
  7.3 377.0 %reduce-scatter.2.cloned.1.call-start = ((), (), s32[]{:S(2)}) async-start(), calls=%async_computation.2 | async-start | bytes 10485760 | tf_op jit(solution)/shard_map/reduce_scatter | solution.py:144
  10.7 2.3 copy-start.7
  12.3 0.7 copy-start.12
  12.4 0.7 copy-start.13
  12.4 0.7 copy-start.14
  12.4 0.6 copy-start.11
  12.4 1.7 copy-start.9
  12.4 1.7 copy-start.10
  18.0 9.2 %copy-start.8 = (s32[512]{0:T(512)S(1)}, s32[512]{0:T(512)}, u32[]{:S(2)}) copy-start(s32[512]{0:T(512)} %copy-done.7) | copy-start | bytes 6148
  18.0 3.6 copy-start
  18.0 3.6 copy-start.6
  24.8 1.3 copy-start.1
  27.2 10.5 %collective-permute-start = (bf16[2,512,128]{2,1,0:T(8,128)(2,1)S(1)}, bf16[2,512,128]{2,1,0:T(8,128)(2,1)S(1)}, u32[]{:S(2)}, u32[]{:S(2)}) collective-permute-start(bf16[2,512,128]{2,1,0:T(8,128)(2,1)S(1)} %get-tuple-element.546), channel_id=1, source_target_pairs={{0,4},{4,8},{8,12},{12,16},{16,20},{20,24},{24,28},{28,32},{32,36}... | collective-permute-start | bytes 786440 | tf_op jit(solution)/shard_map/while/body/eval_jaxpr/ppermute | solution.py:18
  37.7 1.6 copy-start.2
  42.4 2.1 copy-start.3
  44.5 9.3 %collective-permute-start = (bf16[2,512,128]{2,1,0:T(8,128)(2,1)S(1)}, bf16[2,512,128]{2,1,0:T(8,128)(2,1)S(1)}, u32[]{:S(2)}, u32[]{:S(2)}) collective-permute-start(bf16[2,512,128]{2,1,0:T(8,128)(2,1)S(1)} %get-tuple-element.546), channel_id=1, source_target_pairs={{0,4},{4,8},{8,12},{12,16},{16,20},{20,24},{24,28},{28,32},{32,36}... | collective-permute-start | bytes 786440 | tf_op jit(solution)/shard_map/while/body/eval_jaxpr/ppermute | solution.py:18
  53.9 15.6 %collective-permute-start = (bf16[2,512,128]{2,1,0:T(8,128)(2,1)S(1)}, bf16[2,512,128]{2,1,0:T(8,128)(2,1)S(1)}, u32[]{:S(2)}, u32[]{:S(2)}) collective-permute-start(bf16[2,512,128]{2,1,0:T(8,128)(2,1)S(1)} %get-tuple-element.546), channel_id=1, source_target_pairs={{0,4},{4,8},{8,12},{12,16},{16,20},{20,24},{24,28},{28,32},{32,36}... | collective-permute-start | bytes 786440 | tf_op jit(solution)/shard_map/while/body/eval_jaxpr/ppermute | solution.py:18
  69.5 14.6 %collective-permute-start = (bf16[2,512,128]{2,1,0:T(8,128)(2,1)S(1)}, bf16[2,512,128]{2,1,0:T(8,128)(2,1)S(1)}, u32[]{:S(2)}, u32[]{:S(2)}) collective-permute-start(bf16[2,512,128]{2,1,0:T(8,128)(2,1)S(1)} %get-tuple-element.546), channel_id=1, source_target_pairs={{0,4},{4,8},{8,12},{12,16},{16,20},{20,24},{24,28},{28,32},{32,36}... | collective-permute-start | bytes 786440 | tf_op jit(solution)/shard_map/while/body/eval_jaxpr/ppermute | solution.py:18
  302.0 82.3 %copy-start.4 = (bf16[128,8192]{1,0:T(8,128)(2,1)S(1)}, bf16[128,8192]{1,0:T(8,128)(2,1)}, u32[]{:S(2)}) copy-start(bf16[128,8192]{1,0:T(8,128)(2,1)} %param.19) | copy-start | bytes 6291460
Sparse Core Ops, SparseCore 0:
  10.7 274.2 all-gather.1
  302.2 82.0 reduce-scatter.1
where the time goes:
time: 397 us; the launch traced here: 395 us
  waiting for transfers between devices  306 us (77%)
  matrix products  26.2 us (7%)
  other arithmetic  19.4 us (5%)
  starting transfers between devices  15.3 us (4%)
  between operations  14.3 us (4%)
  local copies, waits for them, and re-layouts  10.2 us (3%)
    all_gather x1, waiting for transfers between devices, on_device(): lax.all_gather(out_weight, 'ctx', axis=1, tiled=True)  199 us
    reduce_scatter x1, waiting for transfers between devices, on_device(): lax.psum_scatter(partial_sum.astype(jnp.bfloat16), 'tp', scatter_dimensio...  82.2 us
    ppermute x4, waiting for transfers between devices, from_behind(): return lax.ppermute(block, axis, route)  24.3 us
    dot_general x1, matrix products, on_device(): jnp.dot(attended, lax.all_gather(out_weight, 'ctx', axis=1, tiled=True),...  16.9 us
    ppermute x4, starting transfers between devices, from_behind(): return lax.ppermute(block, axis, route)  15.3 us
  transfers between devices with their start and end apart: 6, of which 6 were waited for; matrix products, arithmetic and copies ran while one was open for 9% of the time, Pallas kernels for 0%

commit v1 on v0

v1 whole, which is shorter than its diff:
```python
import functools
import heapq
import math

import jax
import jax.numpy as jnp
from jax import lax
from jax.experimental import pallas as pl
from jax.experimental.pallas import tpu as pltpu
from jax.sharding import PartitionSpec as P

HD = 128
DOC = 2048
HEADS = 8
TOK = 512
ROWS_A = 480
ROWS_B = 1024 - ROWS_A
NC = 64
BACK = 4
KIB = 1024.0
RATE = 46.6e3 / KIB
HOP = 1.7
PIECE = 0.55
theta_base = 1000000.0
MESH = pl.DeviceIdType.MESH
DZS = (0, 1, -1, 2, -2, 3, -3, 4)


def build_tasks():
    t = {}
    rb, ra = ROWS_B / 4, ROWS_A / 4
    for j in range(1, BACK + 1):
        t[("kv", j)] = ("y+" if j < 3 else "x", 256.0, ())
    t[("h", "b")] = ("x", rb * 2, ())
    t[("h", "a")] = ("x", ra * 2, ())

    def b_has(dz, dh):
        if dz == 0:
            return () if dh == 0 else (("h", "b"),)
        if abs(dz) == 4:
            return (("bz+", 3, dh), ("bz-", 3, dh))
        return (("bz+", dz * -1 - 1, dh),) if dz < 0 else (("bz-", dz - 1, dh),)

    for s in range(4):
        for dh in (0, 1):
            size = rb if s < 3 else rb / 2
            t[("bz+", s, dh)] = ("z+", size, b_has(-s, dh))
            t[("bz-", s, dh)] = ("z-", size, b_has(s, dh))
    for dh in (0, 1):
        t[("ay+", dh)] = ("y+", ra, () if dh == 0 else (("h", "a"),))
        t[("ay-", dh)] = ("y-", ra, () if dh == 0 else (("h", "a"),))
        t[("ar+", dh)] = ("y+", ra / 2, (("ay+", dh),))
        t[("ar-", dh)] = ("y-", ra / 2, (("ay-", dh),))
    column = (("h", "a"),) + tuple((k, dh) for dh in (0, 1) for k in ("ay+", "ay-", "ar+", "ar-"))
    for s in range(4):
        size = ra * 8 if s < 3 else ra * 4
        t[("az+", s)] = ("z+", size, column if s == 0 else (("az+", s - 1),))
        t[("az-", s)] = ("z-", size, column if s == 0 else (("az-", s - 1),))
    for dz in DZS:
        for dh in (0, 1):
            need = b_has(dz, dh)
            t[("by+", dz, dh)] = ("y+", rb, need)
            t[("by-", dz, dh)] = ("y-", rb, need)
            t[("br+", dz, dh)] = ("y+", rb / 2, (("by+", dz, dh),))
            t[("br-", dz, dh)] = ("y-", rb / 2, (("by-", dz, dh),))
    return t


def group_needs(t, dz):
    need = set()
    for dh in (0, 1):
        need |= set(t[("by+", dz, dh)][2])
        need |= {(k, dz, dh) for k in ("by+", "by-", "br+", "br-")}
    if dz == 0:
        need |= set(t[("az+", 0)][2])
    elif dz == 4:
        need |= {("az+", 3), ("az-", 3)}
    else:
        need.add(("az+", -dz - 1) if dz < 0 else ("az-", dz - 1))
    return tuple(sorted(need, key=str))


def plan(t):
    rank = {}
    for n, name in enumerate(t):
        kind = name[0]
        if kind == "kv":
            r = 0
        elif kind == "h":
            r = 1
        elif kind in ("bz+", "bz-"):
            r = 3 + name[1]
        elif kind[0] == "a" and kind[1] in "yr":
            r = 2
        elif kind[:2] == "az":
            r = 10
        else:
            r = 4 + 4 * abs(name[1])
        rank[name] = (r, n)
    link_free = {}
    arrive = {}
    pending = sorted(t, key=lambda k: rank[k])
    order, now = [], 0.0
    computes = [("attn", s, h) for s in range(BACK + 1) for h in range(HEADS)]
    mats = [("M", dz) for dz in DZS]
    sums, finals = [], []
    done = {}
    cost = {"M": 2.0, "S": 0.6, "F": 0.3}

    def needs_of(c):
        if c[0] == "attn":
            return (("kv", c[1]),) if c[1] else ()
        if c[0] == "M":
            return group_needs(t, c[1])
        return ()

    def ready(names):
        return all(arrive.get(n, 1e9) <= now for n in names)

    def send(name, link, size):
        start = max(now, link_free.get(link, 0.0))
        link_free[link] = start + size / RATE
        arrive[name] = link_free[link] + HOP

    while pending or computes or mats or sums or finals:
        moved = [n for n in pending if ready(t[n][2])]
        for n in moved:
            order.append(("send", n))
            send(n, t[n][0], t[n][1])
            pending.remove(n)
        pick = None
        if finals and arrive[("c", finals[0])] <= now and not computes:
            pick = ("F", finals.pop(0))
        elif sums and arrive[("d", sums[0])] <= now:
            pick = ("S", sums.pop(0))
        elif computes and ready(needs_of(computes[0])):
            pick = computes.pop(0)
        elif not computes and mats:
            ok = [c for c in mats if ready(needs_of(c))]
            if ok:
                pick = ok[0]
                mats.remove(pick)
        if pick:
            order.append(pick)
            now += PIECE if pick[0] == "attn" else cost[pick[0]]
            done[pick] = now
            if pick[0] == "M":
                send(("d", pick[1]), "d", 512.0 / 12)
                sums.append(pick[1])
            if pick[0] == "S":
                send(("c", pick[1]), "c", 256.0)
                finals.append(pick[1])
            continue
        later = [a for a in arrive.values() if a > now]
        assert later, "stuck"
        now = min(later) + 1e-6
    return order, now


TASKS = build_tasks()
ORDER, MODEL_US = plan(TASKS)
NAMES = list(TASKS)
NUMBER = {n: i for i, n in enumerate(NAMES)}


def kernel(
    q_hbm, k_hbm, v_hbm, cos_hbm, sin_hbm, segq_ref, segk_ref, w_hbm, res_hbm, out_ref,
    wa, wb, q, cos, sin, kbuf, vbuf, bias, vone, top, acc, att,
    dsend, drecv, keep, other, csend, crecv, res,
    send_sem, recv_sem, dsem, drsem, csem, crsem, kvs2, kvr2, hs2, hr2, local,
):
    c = lax.axis_index("ctx")
    t = lax.axis_index("tp")
    z, h, y = c // 8, (c // 4) % 2, c % 4
    core = t % 2
    chip = t // 2
    mate = chip * 2 + (1 - core)
    across = (1 - chip) * 2 + core

    def at(dz, dh, dy):
        return ((z + dz + 8) % 8) * 8 + ((h + dh) % 2) * 4 + (y + dy + 4) % 4

    def ctx_of(dz, dh, dy):
        return (at(dz, dh, dy), t)

    barrier = pltpu.get_barrier_semaphore()
    partners = [ctx_of(1, 0, 0), ctx_of(-1, 0, 0), ctx_of(0, 0, 1), ctx_of(0, 0, -1),
                ctx_of(0, 1, 0), (c, mate), (c, across)]
    for j in range(1, BACK + 1):
        partners.append(((c + j) % NC, t))
        partners.append(((c - j + NC) % NC, t))
    for d in partners:
        pl.semaphore_signal(barrier, inc=1, device_id=d, device_id_type=MESH)

    loads = {
        "wa": pltpu.make_async_copy(w_hbm.at[pl.ds(0, ROWS_A)], wa.at[c], local.at[0]),
        "wb": pltpu.make_async_copy(w_hbm.at[pl.ds(ROWS_A, ROWS_B)], wb.at[c], local.at[1]),
        "k": pltpu.make_async_copy(k_hbm, kbuf.at[0], local.at[2]),
        "v": pltpu.make_async_copy(v_hbm, vbuf.at[0], local.at[3]),
        "q": pltpu.make_async_copy(q_hbm, q, local.at[4]),
        "cos": pltpu.make_async_copy(cos_hbm, cos, local.at[5]),
        "sin": pltpu.make_async_copy(sin_hbm, sin, local.at[6]),
        "res": pltpu.make_async_copy(res_hbm, res, local.at[7]),
    }
    for k in ("k", "v", "wb", "wa", "q", "cos", "sin", "res"):
        loads[k].start()
    pl.semaphore_wait(barrier, len(partners))
    for k in ("k", "v", "wb", "wa"):
        loads[k].wait()

    half_b = ROWS_B // 2
    half_a = ROWS_A // 2

    def copies(name, incoming):
        kind = name[0]
        n = NUMBER[name]
        sems = (send_sem.at[n], recv_sem.at[n])

        def one(src, dst, dev, pair=sems):
            return pltpu.make_async_remote_copy(
                src_ref=src, dst_ref=dst, send_sem=pair[0], recv_sem=pair[1],
                device_id=dev, device_id_type=MESH)

        def same(ref, dev, pair=sems):
            return one(ref, ref, dev, pair)

        if kind == "kv":
            j = name[1]
            dev = ((c + j) % NC, t)
            return [one(kbuf.at[0], kbuf.at[j], dev),
                    one(vbuf.at[0], vbuf.at[j], dev, (kvs2.at[j - 1], kvr2.at[j - 1]))]
        if kind == "h":
            i = at(0, 1, 0) if incoming else c
            dev = ctx_of(0, 1, 0)
            return [same((wb if name[1] == "b" else wa).at[i], dev)]
        sign = 1 if kind[2] == "+" else -1
        if kind[:2] == "bz":
            s, dh = name[1], name[2]
            i = at(-sign * (s + (1 if incoming else 0)), dh, 0)
            ref = wb.at[i]
            if s == 3:
                ref = wb.at[i, pl.ds(0 if sign > 0 else half_b, half_b)]
            return [same(ref, ctx_of(sign, 0, 0))]
        if kind[:2] == "az":
            s = name[1]
            zz = ((z - sign * (s + (1 if incoming else 0)) + 8) % 8) * 8
            if s < 3:
                ref = wa.at[pl.ds(zz, 8)]
            else:
                ref = wa.at[pl.ds(zz + (0 if sign > 0 else 4), 4)]
            return [same(ref, ctx_of(sign, 0, 0))]
        if kind[0] == "a":
            dz, dh, buf, half = 0, name[1], wa, half_a
        else:
            dz, dh, buf, half = name[1], name[2], wb, half_b
        relay = kind[1] == "r"
        step = (1 if relay else 0) + (1 if incoming else 0)
        i = at(dz, dh, -sign * step)
        ref = buf.at[i]
        if relay:
            ref = buf.at[i, pl.ds(0 if sign > 0 else half, half)]
        return [same(ref, ctx_of(0, 0, sign))]

    got = set()

    def need(names):
        for name in names:
            if name not in got:
                got.add(name)
                for cp in copies(name, True):
                    cp.wait_recv()

    def send(name):
        need(TASKS[name][2])
        for cp in copies(name, False):
            cp.start()

    ready = {"attn": False}
    qk = (((1,), (1,)), ((), ()))
    scale2 = (1.0 / math.sqrt(HD)) * math.log2(math.e)

    def attn_setup(s):
        if s == 0:
            for k in ("q", "cos", "sin"):
                loads[k].wait()
            vone[:, HD:] = jnp.ones((TOK, HD), jnp.bfloat16)
        need((("kv", s),) if s else ())
        segk = segk_ref[pl.ds(BACK - s, 1), :]
        same = segq_ref[...] == segk
        if s == 0:
            row = lax.broadcasted_iota(jnp.int32, (TOK, TOK), 0)
            col = lax.broadcasted_iota(jnp.int32, (TOK, TOK), 1)
            same = same & (col <= row)
        bias[...] = jnp.where(same, 0.0, -1e30).astype(jnp.float32)
        vone[:, :HD] = vbuf[s]

    def attn_piece(s, hd):
        cols = pl.ds(pl.multiple_of(hd * HD, HD), HD)
        if s == 0:
            x = q[:, cols].astype(jnp.float32)
            x = x * cos[...] + pltpu.roll(x, HD // 2, 1) * sin[...]
            qh = x.astype(jnp.bfloat16)
            q[:, cols] = qh
        else:
            qh = q[:, cols]
        score = lax.dot_general(qh, kbuf[s], qk, preferred_element_type=jnp.float32) + bias[...]
        peak = jnp.max(score, axis=1, keepdims=True)
        if s > 0:
            old = top[hd]
            peak = jnp.maximum(peak, old)
        prob = jnp.exp2((score - peak) * scale2).astype(jnp.bfloat16)
        mixed = jnp.dot(prob, vone[...], preferred_element_type=jnp.float32)
        if s > 0:
            mixed = mixed + acc[hd] * jnp.exp2((old - peak) * scale2)
        if s < BACK:
            top[hd] = peak
            acc[hd] = mixed
        else:
            att[:, cols] = (mixed[:, :HD] / mixed[:, HD:]).astype(jnp.bfloat16)

    def group(dz):
        return (z + dz + 8) % 8

    def d_copy(n):
        return pltpu.make_async_remote_copy(
            src_ref=dsend.at[n], dst_ref=drecv.at[n], send_sem=dsem.at[n], recv_sem=drsem.at[n],
            device_id=(c, mate), device_id_type=MESH)

    def c_copy(n):
        return pltpu.make_async_remote_copy(
            src_ref=csend.at[n], dst_ref=crecv.at[n], send_sem=csem.at[n], recv_sem=crsem.at[n],
            device_id=(c, across), device_id_type=MESH)

    def rows_of(tp):
        return pl.ds(pl.multiple_of(tp * 128, 128), 128)

    across_mate = (1 - chip) * 2 + (1 - core)

    def matmul(dz):
        n = DZS.index(dz)
        need(group_needs(TASKS, dz))
        base = group(dz) * 8

        def body(j, carry):
            i = base + 2 * j
            rhs = jnp.concatenate(
                [jnp.concatenate([wa[i], wb[i]], axis=0),
                 jnp.concatenate([wa[i + 1], wb[i + 1]], axis=0)], axis=1)
            cols = pl.ds(pl.multiple_of(j * 256, 256), 256)

            def part(tp):
                return jnp.dot(att[rows_of(tp), :], rhs, preferred_element_type=jnp.float32)

            dsend[n, 0, :, cols] = part(mate).astype(jnp.bfloat16)
            dsend[n, 1, :, cols] = part(across_mate).astype(jnp.bfloat16)
            keep[n, :, cols] = part(t)
            other[n, :, cols] = part(across)
            return carry

        lax.fori_loop(0, 4, body, 0)
        d_copy(n).start()

    def summed(dz):
        n = DZS.index(dz)
        d_copy(n).wait_recv()

        def body(j, carry):
            cols = pl.ds(pl.multiple_of(j * 256, 256), 256)
            csend[n, :, cols] = (
                other[n, :, cols] + drecv[n, 1, :, cols].astype(jnp.float32)).astype(jnp.bfloat16)
            return carry

        lax.fori_loop(0, 4, body, 0)
        c_copy(n).start()

    def final(dz):
        n = DZS.index(dz)
        if n == 0:
            loads["res"].wait()
        c_copy(n).wait_recv()
        first = group(dz) * 1024

        def body(j, carry):
            cols = pl.ds(pl.multiple_of(j * 256, 256), 256)
            wide = pl.ds(pl.multiple_of(first + j * 256, 256), 256)
            total = keep[n, :, cols] + drecv[n, 0, :, cols].astype(jnp.float32)
            total = total + crecv[n, :, cols].astype(jnp.float32)
            out_ref[:, wide] = (total + res[:, wide].astype(jnp.float32)).astype(jnp.bfloat16)
            return carry

        lax.fori_loop(0, 4, body, 0)

    i = 0
    items = ORDER
    while i < len(items):
        item = items[i]
        if item[0] == "attn":
            seg = item[1]
            slots = {}
            hd = -1
            while i < len(items) and (items[i][0] == "send" or items[i][:2] == ("attn", seg)):
                if items[i][0] == "attn":
                    hd = items[i][2]
                else:
                    slots.setdefault(hd, []).append(items[i][1])
                i += 1
            attn_setup(seg)

            def body(hd, carry, seg=seg, slots=slots):
                attn_piece(seg, hd)
                for k, names in slots.items():
                    def issue(names=names):
                        for name in names:
                            send(name)
                    pl.when(hd == k)(issue)
                return carry

            lax.fori_loop(0, HEADS, body, 0)
            continue
        if item[0] == "send":
            send(item[1])
        elif item[0] == "M":
            matmul(item[1])
        elif item[0] == "S":
            summed(item[1])
        else:
            final(item[1])
        i += 1
    for name in NAMES:
        assert name in got, name
        for cp in copies(name, False):
            cp.wait_send()
    for n in range(8):
        d_copy(n).wait_send()
        c_copy(n).wait_send()


def rotary_tables(positions):
    half_dim = HD // 2
    freq_index = jnp.arange(half_dim)
    inv_freq = theta_base ** (-2.0 * freq_index.astype(jnp.float32) / HD)
    first_end = HD // 8
    second_end = first_end + 3 * HD // 16
    place = positions.astype(jnp.float32)
    chosen = jnp.where(
        freq_index[None, :] < first_end,
        place[0][:, None],
        jnp.where(freq_index[None, :] < second_end, place[1][:, None], place[2][:, None]),
    )
    angle = chosen * inv_freq[None, :]
    return (jnp.cos(angle), jnp.sin(angle))


def on_device(queries, keys, values, positions, segment_ids, out_weight, residual):
    cosine, sine = rotary_tables(positions)
    cos2 = jnp.concatenate([cosine, cosine], axis=1)
    sin2 = jnp.concatenate([-sine, sine], axis=1)
    kf = keys.astype(jnp.float32)
    swapped = jnp.concatenate([kf[:, HD // 2:], kf[:, :HD // 2]], axis=1)
    rot_k = (kf * cos2 + swapped * sin2).astype(jnp.bfloat16)
    my = lax.axis_index("ctx")
    wrapped = jnp.concatenate([segment_ids[-BACK * TOK:], segment_ids])
    window = lax.dynamic_slice_in_dim(wrapped, my * TOK, (BACK + 1) * TOK, 0)
    segk = jnp.concatenate(
        [window.reshape(BACK + 1, TOK), jnp.zeros((7 - BACK, TOK), jnp.int32)], axis=0)
    segq = window[BACK * TOK:].reshape(TOK, 1)
    anyspec = pl.BlockSpec(memory_space=pl.ANY)
    vmem = pl.BlockSpec(memory_space=pltpu.VMEM)
    nt = len(NAMES)
    bf, f32 = jnp.bfloat16, jnp.float32
    return pl.pallas_call(
        kernel,
        out_shape=jax.ShapeDtypeStruct((128, 8192), bf),
        in_specs=[anyspec] * 5 + [vmem] * 2 + [anyspec] * 2,
        out_specs=vmem,
        scratch_shapes=[
            pltpu.VMEM((NC, ROWS_A, 128), bf),
            pltpu.VMEM((NC, ROWS_B, 128), bf),
            pltpu.VMEM((TOK, 1024), bf),
            pltpu.VMEM((TOK, HD), f32),
            pltpu.VMEM((TOK, HD), f32),
            pltpu.VMEM((BACK + 1, TOK, HD), bf),
            pltpu.VMEM((BACK + 1, TOK, HD), bf),
            pltpu.VMEM((TOK, TOK), f32),
            pltpu.VMEM((TOK, 2 * HD), bf),
            pltpu.VMEM((HEADS, TOK, 1), f32),
            pltpu.VMEM((HEADS, TOK, 2 * HD), f32),
            pltpu.VMEM((TOK, 1024), bf),
            pltpu.VMEM((8, 2, 128, 1024), bf),
            pltpu.VMEM((8, 2, 128, 1024), bf),
            pltpu.VMEM((8, 128, 1024), f32),
            pltpu.VMEM((8, 128, 1024), f32),
            pltpu.VMEM((8, 128, 1024), bf),
            pltpu.VMEM((8, 128, 1024), bf),
            pltpu.VMEM((128, 8192), bf),
            pltpu.SemaphoreType.DMA((nt,)),
            pltpu.SemaphoreType.DMA((nt,)),
            pltpu.SemaphoreType.DMA((8,)),
            pltpu.SemaphoreType.DMA((8,)),
            pltpu.SemaphoreType.DMA((8,)),
            pltpu.SemaphoreType.DMA((8,)),
            pltpu.SemaphoreType.DMA((BACK,)),
            pltpu.SemaphoreType.DMA((BACK,)),
            pltpu.SemaphoreType.DMA((1,)),
            pltpu.SemaphoreType.DMA((1,)),
            pltpu.SemaphoreType.DMA((8,)),
        ],
        compiler_params=pltpu.CompilerParams(
            collective_id=0, has_side_effects=True, vmem_limit_bytes=62 * 1024 * 1024),
    )(queries, rot_k, values, cos2, sin2, segq, segk, out_weight, residual)


def solution(mesh):
    return jax.shard_map(
        on_device,
        mesh=mesh,
        in_specs=(
            P("ctx", "tp"),
            P("ctx", "tp"),
            P("ctx", "tp"),
            P(None, "ctx"),
            P(),
            P("tp", "ctx"),
            P(("ctx", "tp"), None),
        ),
        out_specs=P(("ctx", "tp"), None),
        check_vma=False,
    )
```

time: 397 us -> 222 us (0.56)
  the two profiles are of different devices: /device:TPU:15 before, /device:TPU:4 now
where the time goes in v1:
time: 222 us
  Pallas kernels  211 us (95%)
  local copies, waits for them, and re-layouts  6.37 us (3%)
  other arithmetic  4.35 us (2%)
    pallas_call x1, Pallas kernels, on_device(): pl.pallas_call(kernel, out_shape=jax.ShapeDtypeStruct((128, 8192), bf), i...  211 us

profile of v1, /device:TPU:4, one launch (start us, length us, event | category | flops | bytes accessed | tf_op | source)
XLA Modules:
  0.0 221.8 jit_solution(6788164177457339129)
XLA Ops:
  0.0 0.0 copy-start
  0.0 0.7 convert_element_type.17
  0.8 0.7 slice.26
  1.5 0.8 fusion.5
  2.3 0.6 concatenate.19.segk_ref
  2.9 0.9 copy.8.segq_ref
  3.7 1.1 fusion.6
  4.8 1.7 fusion.4
  6.5 0.0 copy-done
  6.6 1.1 fusion.1
  7.7 211.1 %shard_map.73 = bf16[128,8192]{1,0:T(8,128)(2,1)} custom-call(bf16[512,1024]{1,0:T(8,128)(2,1)} %q_hbm.1, bf16[512,128]{1,0:T(8,128)(2,1)} %get-tuple-element.5.k_hbm, bf16[512,128]{1,0:T(8,128)(2,1)} %v_hbm.1, f32[512,128]{1,0:T(8,128)} %get-tuple-element.7.cos_hbm, f32[512,128]{1,0:T(8,128)} %get-tuple-element.6.sin_hbm, s32[512,1]{1,0:T(8,128)} %copy.8.segq_ref, ...), custom_call_target="tpu_custom_call" | custom-call | tf_op jit(solution)/shard_map/pallas_call | solution.py:471
  218.7 3.1 %copy.10 = bf16[128,8192]{1,0:T(8,128)(2,1)} copy(bf16[128,8192]{1,0:T(8,128)(2,1)} %shard_map.73) | data formatting | bytes 4194304
  (5 shorter events, 0.0 us)
Async XLA Ops:
  0.0 6.5 %copy-start = (bf16[512,128]{1,0:T(8,128)(2,1)S(1)}, bf16[512,128]{1,0:T(8,128)(2,1)}, u32[]{:S(2)}) copy-start(bf16[512,128]{1,0:T(8,128)(2,1)} %param.8) | copy-start | bytes 393220

commit v2 on v1

--- a/solution.py
+++ b/solution.py
@@ -21,6 +21,7 @@
 RATE = 46.6e3 / KIB
 HOP = 1.7
 PIECE = 0.55
+AHEAD = 4.0
 theta_base = 1000000.0
 MESH = pl.DeviceIdType.MESH
 DZS = (0, 1, -1, 2, -2, 3, -3, 4)
@@ -84,14 +85,14 @@
     rank = {}
     for n, name in enumerate(t):
         kind = name[0]
-        if kind == "kv":
-            r = 0
-        elif kind == "h":
+        if kind == "h":
+            r = 0 if name[1] == "a" else 2
+        elif kind[0] == "a" and kind[1] in "yr":
             r = 1
+        elif kind == "kv":
+            r = 2
         elif kind in ("bz+", "bz-"):
             r = 3 + name[1]
-        elif kind[0] == "a" and kind[1] in "yr":
-            r = 2
         elif kind[:2] == "az":
             r = 10
         else:
@@ -123,11 +124,11 @@
         arrive[name] = link_free[link] + HOP
 
     while pending or computes or mats or sums or finals:
-        moved = [n for n in pending if ready(t[n][2])]
-        for n in moved:
-            order.append(("send", n))
-            send(n, t[n][0], t[n][1])
-            pending.remove(n)
+        for n in list(pending):
+            if ready(t[n][2]) and link_free.get(t[n][0], 0.0) - now < AHEAD:
+                order.append(("send", n))
+                send(n, t[n][0], t[n][1])
+                pending.remove(n)
         pick = None
         if finals and arrive[("c", finals[0])] <= now and not computes:
             pick = ("F", finals.pop(0))
@@ -152,6 +153,7 @@
                 finals.append(pick[1])
             continue
         later = [a for a in arrive.values() if a > now]
+        later += [f - AHEAD for f in link_free.values() if f - AHEAD > now]
         assert later, "stuck"
         now = min(later) + 1e-6
     return order, now

time: 222 us -> 175 us (0.79)
  the two profiles are of different devices: /device:TPU:4 before, /device:TPU:15 now
where the time goes in v2:
time: 175 us; the launch traced here: 171 us
  Pallas kernels  161 us (92%)
  local copies, waits for them, and re-layouts  6.37 us (4%)
  other arithmetic  4.35 us (2%)
    pallas_call x1, Pallas kernels, on_device(): pl.pallas_call(kernel, out_shape=jax.ShapeDtypeStruct((128, 8192), bf), i...  161 us

profile of v2, /device:TPU:15, one launch (start us, length us, event | category | flops | bytes accessed | tf_op | source)
XLA Modules:
  0.0 171.5 jit_solution(8967391778914217366)
XLA Ops:
  0.0 0.0 copy-start
  0.0 0.7 convert_element_type.17
  0.8 0.7 slice.26
  1.5 0.8 fusion.5
  2.3 0.6 concatenate.19.segk_ref
  2.9 0.9 copy.8.segq_ref
  3.7 1.1 fusion.6
  4.8 1.7 fusion.4
  6.5 0.0 copy-done
  6.6 1.1 fusion.1
  7.7 160.7 %shard_map.73 = bf16[128,8192]{1,0:T(8,128)(2,1)} custom-call(bf16[512,1024]{1,0:T(8,128)(2,1)} %q_hbm.1, bf16[512,128]{1,0:T(8,128)(2,1)} %get-tuple-element.5.k_hbm, bf16[512,128]{1,0:T(8,128)(2,1)} %v_hbm.1, f32[512,128]{1,0:T(8,128)} %get-tuple-element.7.cos_hbm, f32[512,128]{1,0:T(8,128)} %get-tuple-element.6.sin_hbm, s32[512,1]{1,0:T(8,128)} %copy.8.segq_ref, ...), custom_call_target="tpu_custom_call" | custom-call | tf_op jit(solution)/shard_map/pallas_call | solution.py:473
  168.4 3.1 %copy.10 = bf16[128,8192]{1,0:T(8,128)(2,1)} copy(bf16[128,8192]{1,0:T(8,128)(2,1)} %shard_map.73) | data formatting | bytes 4194304
  (5 shorter events, 0.0 us)
Async XLA Ops:
  0.0 6.5 %copy-start = (bf16[512,128]{1,0:T(8,128)(2,1)S(1)}, bf16[512,128]{1,0:T(8,128)(2,1)}, u32[]{:S(2)}) copy-start(bf16[512,128]{1,0:T(8,128)(2,1)} %param.8) | copy-start | bytes 393220

commit v3 on v0

v3 whole, which is shorter than its diff:
```python
import math

import jax
import jax.numpy as jnp
from jax import lax
from jax.experimental import pallas as pl
from jax.experimental.pallas import tpu as pltpu
from jax.sharding import PartitionSpec as P

HD = 128
HEADS = 8
TOK = 512
CHUNK = 128
BACK = 4
SPAN = (BACK + 1) * TOK
WINDOW = BACK * TOK + CHUNK
ROWS_A = 512
ROWS_B = 1024 - ROWS_A
RATE = 45.5
HOP = 1.9
STEP = 3.0
AHEAD = 6.0
BIG = 2.0**100
theta_base = 1000000.0
MESH = pl.DeviceIdType.MESH
PARTS = ((0, 1, -1, 2), (-2, 3, -3, 4))
NEAR = (0, 1, 2, -1)


def build_tasks():
    t = {}
    ra, rb = float(ROWS_A), float(ROWS_B)
    for j in range(1, BACK + 1):
        t[("kv", j)] = ("y+" if j < 3 else "x+", 256.0, (), 2.0)
    for k, rows in (("a", ra), ("b", rb)):
        t[("tg", k)] = ("x-", rows / 4, (), 1.0)
    for half in (0, 1):
        t[("ay+", half)] = ("y+", ra / 4, (("tg", "a"),), 0.0)
        t[("ay-", half)] = ("y-", ra / 4, (("tg", "a"),), 0.0)
    t[("ar+", 0)] = ("y+", ra / 4, (("ay+", 0),), 0.0)
    t[("ar-", 1)] = ("y-", ra / 4, (("ay-", 1),), 0.0)
    for p in range(4):
        for s, order in (("+", p), ("-", 3 - p)):
            t[("bs" + s, order)] = ("z" + s, rb / 4, (("tg", "b"),), 0.0)
            t[("br" + s, order)] = ("z" + s, 1.0, (("bs" + s, order),), 2 * HOP)
    column = (("tg", "a"), ("ay+", 0), ("ay+", 1), ("ay-", 0), ("ay-", 1), ("ar+", 0), ("ar-", 1))
    for s in range(4):
        size = ra if s < 3 else ra / 2
        t[("az+", s)] = ("z+", size, column if s == 0 else (("az+", s - 1),), 0.0)
        t[("az-", s)] = ("z-", size, column if s == 0 else (("az-", s - 1),), 0.0)
    for slot in "NF":
        for half in (0, 1):
            pieces = (2 * half, 2 * half + 1)
            kind = "bs" if slot == "N" else "br"
            need = (("tg", "b"),) + tuple((kind + s, p) for s in "+-" for p in pieces)
            t[("by+", slot, half)] = ("y+", rb / 2, need, 0.0)
            t[("by-", slot, half)] = ("y-", rb / 2, need, 0.0)
        t[("bq+", slot, 0)] = ("y+", rb / 2, (("by+", slot, 0),), 0.0)
        t[("bq-", slot, 1)] = ("y-", rb / 2, (("by-", slot, 1),), 0.0)
    for m in range(4):
        for s in "+-":
            t[("at" + s, m)] = ("x" + s, 256.0, (("att", m),), 0.0)
            t[("ar2" + s, m)] = ("x" + s, 128.0, (("at" + s, m),), 0.0)
        t[("am", m, "own")] = ("d", 256.0 / 12, (("att", m),), 0.0)
        for s in "+-":
            t[("am", m, s)] = ("d", 256.0 / 12, (("at" + s, m),), 0.0)
            t[("am", m, s + "2")] = ("d", 128.0 / 12, (("ar2" + s, m),), 0.0)
    return t


def b_names(slots):
    out = []
    for slot in slots:
        for half in (0, 1):
            out += [("by+", slot, half), ("by-", slot, half)]
        out += [("bq+", slot, 0), ("bq-", slot, 1)]
    return out


def mat_needs(m, part):
    need = [("am", m, k) for k in ("own", "+", "-", "+2", "-2")]
    need += [("at+", m), ("at-", m), ("ar2+", m), ("ar2-", m)]
    need += b_names("N" if part == 0 else "NF")
    deep = 2 if part == 0 else 4
    for s in range(deep):
        need += [("az+", s), ("az-", s)]
    return tuple(need)


def plan(t):
    rank = {}
    for n, name in enumerate(t):
        k = name[0]
        if k == "kv":
            r = 1
        elif k == "tg":
            r = 0
        elif k in ("ay+", "ay-", "ar+", "ar-"):
            r = 2
        elif k in ("bs+", "bs-", "br+", "br-"):
            r = 3
        elif k in ("az+", "az-"):
            r = 6
        elif k in ("at+", "at-"):
            r = 4
        elif k in ("ar2+", "ar2-"):
            r = 3
        elif k == "am":
            r = 4
        else:
            r = 5 if name[1] == "N" else 7
        rank[name] = (r, n)
    link_free, arrive = {}, {}
    pending = sorted(t, key=lambda k: rank[k])
    order, now = [], 0.0
    steps = [(m, g) for m in range(4) for g in range(2)]
    mats = [(m, part) for part in range(2) for m in range(4)]
    finals = []
    sent = {0: [], 1: []}

    def ready(names):
        return all(arrive.get(n, 1e9) <= now for n in names)

    def send(name, link, size, extra):
        start = max(now, link_free.get(link, 0.0))
        link_free[link] = start + size / RATE
        arrive[name] = link_free[link] + HOP + extra

    while pending or steps or mats or finals:
        for n in list(pending):
            if ready(t[n][2]) and link_free.get(t[n][0], 0.0) - now < AHEAD:
                order.append(("send", n))
                send(n, *[t[n][i] for i in (0, 1, 3)])
                pending.remove(n)
        if steps:
            if ready([("kv", j) for j in range(1, BACK + 1)]):
                m, g = steps.pop(0)
                order.append(("step", m, g))
                now += STEP
                if g == 1:
                    arrive[("att", m)] = now
                continue
        elif mats:
            ok = [c for c in mats if ready(mat_needs(*c))]
            if ok:
                m, part = ok[0]
                mats.remove(ok[0])
                order.append(("M", m, part))
                now += 1.5
                send(("c", m, part), "x+", 140.0, 1.0)
                sent[part].append(("c", m, part))
                if len(sent[part]) == 4:
                    finals.append(part)
                continue
        if finals and not steps and ready(sent[finals[0]]):
            order.append(("F", finals.pop(0)))
            now += 1.0
            continue
        later = [a for a in arrive.values() if a > now]
        later += [f - AHEAD for f in link_free.values() if f - AHEAD > now]
        assert later, "stuck"
        now = min(later) + 1e-6
    return order, now, arrive


TASKS = build_tasks()
ORDER, MODEL_US, ARRIVE = plan(TASKS)
NAMES = list(TASKS)
NUMBER = {n: i for i, n in enumerate(NAMES)}


def kernel(
    q_hbm, k_hbm, v_hbm, cos_hbm, sin_hbm, hot_hbm, w_hbm, res_hbm, out_ref,
    wa, wb, q, cos, sin, kbuf, vbuf, hot, att, csend, crecv, res,
    send_sem, recv_sem, kv_send, kv_recv, tg_recv, c_send, c_recv, local,
):
    c = lax.axis_index("ctx")
    t = lax.axis_index("tp")
    z, h, y = c // 8, (c // 4) % 2, c % 4
    core = t % 2
    chip = t // 2
    x = h * 2 + chip
    owner = (z + y) % 4
    r = (t - z - y + 16) % 4
    me = h * 4 + t

    def ctx_of(dz, dh, dy):
        return (((z + dz + 8) % 8) * 8 + ((h + dh) % 2) * 4 + (y + dy + 4) % 4, t)

    def ring(d):
        other = (x + d + 4) % 4
        return (z * 8 + (other // 2) * 4 + y, (other % 2) * 2 + core)

    mate = (c, chip * 2 + (1 - core))
    barrier = pltpu.get_barrier_semaphore()
    partners = [ctx_of(1, 0, 0), ctx_of(-1, 0, 0), ctx_of(0, 0, 1), ctx_of(0, 0, -1)]
    for d in range(4):
        for k in range(2):
            other = (x + d) % 4
            who = (z * 8 + (other // 2) * 4 + y, (other % 2) * 2 + (core + k) % 2)
            if d or k:
                partners.append(who)
    for j in range(1, BACK + 1):
        partners.append(((c + j) % 64, t))
        partners.append(((c - j + 64) % 64, t))
    for d in partners:
        pl.semaphore_signal(barrier, inc=1, device_id=d, device_id_type=MESH)

    own = pl.ds(BACK * TOK, TOK)
    loads = {
        "k": pltpu.make_async_copy(k_hbm, kbuf.at[own], local.at[0]),
        "v": pltpu.make_async_copy(v_hbm, vbuf.at[own], local.at[1]),
        "q": pltpu.make_async_copy(q_hbm, q, local.at[2]),
        "cos": pltpu.make_async_copy(cos_hbm, cos, local.at[3]),
        "sin": pltpu.make_async_copy(sin_hbm, sin, local.at[4]),
        "hot": pltpu.make_async_copy(hot_hbm, hot, local.at[5]),
        "res": pltpu.make_async_copy(res_hbm, res, local.at[6]),
    }
    for cp in loads.values():
        cp.start()
    w_rows = {"a": pl.ds(0, ROWS_A), "b": pl.ds(ROWS_A, ROWS_B)}
    w_buf = {"a": wa, "b": wb}
    w_local = {
        k: pltpu.make_async_copy(w_hbm.at[w_rows[k]], w_buf[k].at[z, t], local.at[7 + i])
        for i, k in enumerate("ab")
    }

    @pl.when(owner == t)
    def _():
        for k in "ab":
            w_local[k].start()

    with jax.named_scope("barrier"):
        pl.semaphore_wait(barrier, len(partners))
    with jax.named_scope("kvload"):
        loads["k"].wait()
        loads["v"].wait()

    def slot(which, dy):
        rr = (r - dy + 8) % 4
        near = jnp.where(rr == 3, -1, rr)
        return (z + near + (8 if which == "N" else 12)) % 8

    def halves(half):
        return pl.ds(2 * half, 2)

    def copies(name, incoming):
        kind = name[0]
        n = NUMBER.get(name)

        def one(src, dst, dev, ss=None, rs=None):
            return pltpu.make_async_remote_copy(
                src_ref=src, dst_ref=dst,
                send_sem=send_sem.at[n] if ss is None else ss,
                recv_sem=recv_sem.at[n] if rs is None else rs,
                device_id=dev, device_id_type=MESH)

        def same(ref, dev, **k):
            return one(ref, ref, dev, **k)

        if kind == "kv":
            j = name[1]
            dev = ((c + j) % 64, t)
            to = pl.ds((BACK - j) * TOK, TOK)
            return [(None, one(kbuf.at[own], kbuf.at[to], dev)),
                    (None, one(vbuf.at[own], vbuf.at[to], dev, kv_send.at[j - 1], kv_recv.at[j - 1]))]
        if kind == "tg":
            k = name[1]
            i = "ab".index(k)
            if not incoming:
                return [(owner != t, one(w_hbm.at[w_rows[k]], w_buf[k].at[z, t], (c, owner),
                                         rs=tg_recv.at[i, t]))]
            return [((r == 0) & (t != u),
                     same(w_buf[k].at[z, u], (c, owner), rs=tg_recv.at[i, u])) for u in range(4)]
        if kind in ("at+", "at-", "ar2+", "ar2-", "am"):
            m = name[1]
            rows = pl.ds(m * CHUNK, CHUNK)
            if kind == "am":
                k = name[2]
                d = {"own": 0, "+": -1, "-": 1, "+2": 2, "-2": 2}[k]
                from_core = (1 - core) if incoming else core
                if k == "+2":
                    rows = pl.ds(m * CHUNK, CHUNK // 2)
                if k == "-2":
                    rows = pl.ds(m * CHUNK + CHUNK // 2, CHUNK // 2)
                i = ((x + d + 4) % 4) * 2 + from_core
                return [(None, same(att.at[i, rows], mate))]
            sign = 1 if kind[-1] == "+" else -1
            d = -sign * ((1 if kind[:3] == "ar2" else 0) + (1 if incoming else 0))
            if kind[:3] == "ar2":
                rows = pl.ds(m * CHUNK + (0 if sign > 0 else CHUNK // 2), CHUNK // 2)
            i = ((x + d + 4) % 4) * 2 + core
            return [(None, same(att.at[i, rows], ring(sign)))]
        sign = 1 if kind[2] == "+" else -1
        if kind[:2] in ("ay", "ar"):
            half = name[1]
            ref = wa.at[z, halves(half)]
            if kind[:2] == "ay":
                cond = (r == (3 if sign > 0 else 1)) if incoming else (r == 0)
            else:
                cond = (r == 2) if incoming else (r == (3 if sign > 0 else 1))
            return [(cond, same(ref, ctx_of(0, 0, sign)))]
        if kind[:2] == "az":
            s = name[1]
            zz = (z - sign * (s + (1 if incoming else 0)) + 8) % 8
            ref = wa.at[zz] if s < 3 else wa.at[zz, halves(0 if sign > 0 else 1)]
            return [(None, same(ref, ctx_of(sign, 0, 0)))]
        if kind[:2] in ("bs", "br", "bz"):
            p = name[1]
            far = (4 - r) % 4 if sign > 0 else r
            n = NUMBER[("bs" + kind[2], p)]
            carried = p < 2 if sign > 0 else p >= 2
            last = 1 if sign > 0 else 3
            if not incoming:
                zs = (z - sign * far + 8) % 8
                if kind[:2] == "bs":
                    cond = r == 0
                else:
                    cond = (r != 0) if carried else ((r != 0) & (r != last))
                return [(cond, same(wb.at[zs, p], ctx_of(sign, 0, 0)))]
            zs = (z - sign * ((far + 3) % 4 + 1) + 16) % 8
            cp = same(wb.at[zs, p], ctx_of(sign, 0, 0))
            near = (r == 3) if sign > 0 else ((r == 1) | (r == 2))
            if kind[:2] == "bs":
                return [(near, cp)]
            far_end = (r != 0) & jnp.logical_not(near)
            return [(far_end if kind[:2] == "br" else r == 0, cp)]
        which, half = name[1], name[2]
        step = (1 if kind[:2] == "bq" else 0) + (1 if incoming else 0)
        zs = slot(which, -sign * step)
        return [(None, same(wb.at[zs, halves(half)], ctx_of(0, 0, sign)))]

    def under(cond, act):
        if cond is None:
            act()
        else:
            pl.when(cond)(act)

    got = set()

    def need(names):
        for name in names:
            if name not in got and name[0] != "att":
                got.add(name)
                if name[0] == "tg":
                    @pl.when(owner == t)
                    def _(name=name):
                        w_local[name[1]].wait()
                for cond, cp in copies(name, True):
                    under(cond, cp.wait_recv)

    def send(name):
        need(TASKS[name][2])
        if name[0] in ("br+", "br-"):
            need([name])
        if name[0] in ("by+", "by-") and name[1] == "F":
            need([("bz+", p) for p in (0, 1)] if name[2] == 0 else [("bz-", p) for p in (2, 3)])
        for cond, cp in copies(name, False):
            under(cond, cp.start)

    scale2 = (1.0 / math.sqrt(HD)) * math.log2(math.e)

    def rotate_queries():
        for k in ("q", "cos", "sin", "hot"):
            loads[k].wait()

        def body(hd, carry):
            cols = pl.ds(pl.multiple_of(hd * HD, HD), HD)
            v = q[:, cols].astype(jnp.float32)
            v = v * cos[...] + pltpu.roll(v, HD // 2, 1) * sin[...]
            q[:, cols] = v.astype(jnp.bfloat16)
            return carry

        lax.fori_loop(0, HEADS, body, 0)

    def attend(m, g):
        rows = pl.ds(pl.multiple_of(m * CHUNK, CHUNK), CHUNK)
        keys = pl.ds(pl.multiple_of(m * CHUNK, CHUNK), WINDOW)
        mine = hot[pl.ds(pl.multiple_of(BACK * TOK + m * CHUNK, CHUNK), CHUNK), :]
        heads = []
        for i in range(4):
            qh = q[rows, pl.ds(pl.multiple_of((g * 4 + i) * HD, HD), HD)]
            heads.append(jnp.concatenate([qh, mine], axis=1))
        qs = jnp.concatenate(heads, axis=0)
        other = ((hot[keys, :].astype(jnp.float32) - 1.0) * BIG).astype(jnp.bfloat16)
        ks = jnp.concatenate([kbuf[keys, :], other], axis=1)
        score = lax.dot_general(
            qs, ks, (((1,), (1,)), ((), ())), preferred_element_type=jnp.float32)
        row = lax.broadcasted_iota(jnp.int32, (4 * CHUNK, CHUNK), 0) % CHUNK
        col = lax.broadcasted_iota(jnp.int32, (4 * CHUNK, CHUNK), 1)
        edge = jnp.where(col <= row, score[:, WINDOW - CHUNK:], -BIG)
        score = jnp.concatenate([score[:, :WINDOW - CHUNK], edge], axis=1)
        peak = jnp.max(score, axis=1, keepdims=True)
        prob = jnp.exp2((score - peak) * scale2).astype(jnp.bfloat16)
        vs = jnp.concatenate([vbuf[keys, :], jnp.ones((WINDOW, HD), jnp.bfloat16)], axis=1)
        mixed = jnp.dot(prob, vs, preferred_element_type=jnp.float32)
        result = (mixed[:, :HD] / mixed[:, HD:]).astype(jnp.bfloat16)
        for i in range(4):
            att[me, rows, pl.ds(pl.multiple_of((g * 4 + i) * HD, HD), HD)] = (
                result[i * CHUNK:(i + 1) * CHUNK])

    def c_copy(m, hh, part):
        return pltpu.make_async_remote_copy(
            src_ref=csend.at[m, hh, part], dst_ref=crecv.at[me, part],
            send_sem=c_send.at[m, hh, part], recv_sem=c_recv.at[me, part],
            device_id=(z * 8 + hh * 4 + y, m), device_id_type=MESH)

    def matmul(m, part):
        need(mat_needs(m, part))
        rows = pl.ds(m * CHUNK, CHUNK)
        for pair in range(2):
            total = None
            z0, z1 = [(z + PARTS[part][2 * pair + i] + 8) % 8 for i in range(2)]
            for u in range(4):
                lhs = jnp.concatenate([att[u, rows, :], att[4 + u, rows, :]], axis=0)
                rhs = jnp.concatenate(
                    [jnp.concatenate([wa[z0, u], wb[z0, u]], axis=0),
                     jnp.concatenate([wa[z1, u], wb[z1, u]], axis=0)], axis=1)
                one = jnp.dot(lhs, rhs, preferred_element_type=jnp.float32)
                total = one if total is None else total + one
            total = total.astype(jnp.bfloat16)
            cols = pl.ds(pair * 256, 256)
            for hh in range(2):
                csend[m, hh, part, :, cols] = total[hh * CHUNK:(hh + 1) * CHUNK]
        for hh in range(2):
            mine = (h == hh) & (t == m)

            @pl.when(mine)
            def _(hh=hh):
                crecv[me, part] = csend[m, hh, part]

            pl.when(jnp.logical_not(mine))(c_copy(m, hh, part).start)

    def final(part):
        if part == 0:
            loads["res"].wait()

        def body(s, carry):
            hs, ts = s // 4, s % 4
            cp = pltpu.make_async_remote_copy(
                src_ref=csend.at[0, 0, part], dst_ref=crecv.at[s, part],
                send_sem=c_send.at[0, 0, part], recv_sem=c_recv.at[s, part],
                device_id=mate, device_id_type=MESH)
            pl.when(s != me)(cp.wait_recv)
            for i, dz in enumerate(PARTS[part]):
                zs = (z + dz + 8) % 8
                col = (zs * 8 + hs * 4 + (ts - zs + 8) % 4) * HD
                wide = pl.ds(pl.multiple_of(col, HD), HD)
                got_c = crecv[s, part, :, i * HD:(i + 1) * HD].astype(jnp.float32)
                out_ref[:, wide] = (got_c + res[:, wide].astype(jnp.float32)).astype(jnp.bfloat16)
            return carry

        lax.fori_loop(0, 8, body, 0)

    items = list(ORDER)
    first = next(i for i, it in enumerate(items) if it[0] == "step")
    last = max(i for i, it in enumerate(items) if it[0] == "step")
    rotated = False
    for it in items[:first]:
        if not rotated and it[1][0] not in ("tg", "kv"):
            rotated = True
            with jax.named_scope("rotq"):
                rotate_queries()
        with jax.named_scope("s_" + "_".join(map(str, it[1])).replace("+", "p").replace("-", "m")):
            send(it[1])
    need([("kv", j) for j in range(1, BACK + 1)])
    slots, at_step = {}, -1
    for it in items[first:last + 1]:
        if it[0] == "step":
            at_step += 1
        else:
            slots.setdefault(at_step, []).append(it[1])

    def step(i, carry):
        with jax.named_scope("attend"):
            attend(i // 2, i % 2)
        for k, names in slots.items():
            def issue(names=names):
                for name in names:
                    send(name)
            pl.when(i == k)(issue)
        return carry

    lax.fori_loop(0, 8, step, 0)
    for it in items[last + 1:]:
        if it[0] == "send":
            with jax.named_scope("s_" + "_".join(map(str, it[1])).replace("+", "p").replace("-", "m")):
                send(it[1])
        elif it[0] == "M":
            with jax.named_scope("M%d%d" % it[1:]):
                matmul(*it[1:])
        else:
            with jax.named_scope("F%d" % it[1]):
                final(it[1])
    for name in NAMES:
        need([name])
        for cond, cp in copies(name, False):
            under(cond, cp.wait_send)
    for m in range(4):
        for hh in range(2):
            for part in range(2):
                pl.when(jnp.logical_not((h == hh) & (t == m)))(c_copy(m, hh, part).wait_send)


def rotary_tables(positions):
    half_dim = HD // 2
    freq_index = jnp.arange(half_dim)
    inv_freq = theta_base ** (-2.0 * freq_index.astype(jnp.float32) / HD)
    first_end = HD // 8
    second_end = first_end + 3 * HD // 16
    place = positions.astype(jnp.float32)
    chosen = jnp.where(
        freq_index[None, :] < first_end,
        place[0][:, None],
        jnp.where(freq_index[None, :] < second_end, place[1][:, None], place[2][:, None]),
    )
    angle = chosen * inv_freq[None, :]
    return (jnp.cos(angle), jnp.sin(angle))


def on_device(queries, keys, values, positions, segment_ids, out_weight, residual):
    cosine, sine = rotary_tables(positions)
    cos2 = jnp.concatenate([cosine, cosine], axis=1)
    sin2 = jnp.concatenate([-sine, sine], axis=1)
    kf = keys.astype(jnp.float32)
    swapped = jnp.concatenate([kf[:, HD // 2:], kf[:, :HD // 2]], axis=1)
    rot_k = (kf * cos2 + swapped * sin2).astype(jnp.bfloat16)
    my = lax.axis_index("ctx")
    wrapped = jnp.concatenate([segment_ids[-BACK * TOK:], segment_ids])
    window = lax.dynamic_slice_in_dim(wrapped, my * TOK, SPAN, 0)
    hot = (window[:, None] == jnp.arange(HD, dtype=jnp.int32)[None, :]).astype(jnp.bfloat16)
    anyspec = pl.BlockSpec(memory_space=pl.ANY)
    nt = len(NAMES)
    bf, f32 = jnp.bfloat16, jnp.float32
    dma = pltpu.SemaphoreType.DMA
    return pl.pallas_call(
        kernel,
        out_shape=jax.ShapeDtypeStruct((CHUNK, 8192), bf),
        in_specs=[anyspec] * 8,
        out_specs=pl.BlockSpec(memory_space=pltpu.VMEM),
        scratch_shapes=[
            pltpu.VMEM((8, 4, ROWS_A, HD), bf),
            pltpu.VMEM((8, 4, ROWS_B, HD), bf),
            pltpu.VMEM((TOK, 1024), bf),
            pltpu.VMEM((TOK, HD), f32),
            pltpu.VMEM((TOK, HD), f32),
            pltpu.VMEM((SPAN, HD), bf),
            pltpu.VMEM((SPAN, HD), bf),
            pltpu.VMEM((SPAN, HD), bf),
            pltpu.VMEM((8, TOK, 1024), bf),
            pltpu.VMEM((4, 2, 2, CHUNK, 512), bf),
            pltpu.VMEM((8, 2, CHUNK, 512), bf),
            pltpu.VMEM((CHUNK, 8192), bf),
            dma((nt,)),
            dma((nt,)),
            dma((BACK,)),
            dma((BACK,)),
            dma((2, 4)),
            dma((4, 2, 2)),
            dma((8, 2)),
            dma((9,)),
        ],
        compiler_params=pltpu.CompilerParams(
            collective_id=0, has_side_effects=True, vmem_limit_bytes=62 * 1024 * 1024),
    )(queries, rot_k, values, cos2, sin2, hot, out_weight, residual)


def solution(mesh):
    return jax.shard_map(
        on_device,
        mesh=mesh,
        in_specs=(
            P("ctx", "tp"),
            P("ctx", "tp"),
            P("ctx", "tp"),
            P(None, "ctx"),
            P(),
            P("tp", "ctx"),
            P(("ctx", "tp"), None),
        ),
        out_specs=P(("ctx", "tp"), None),
        check_vma=False,
    )
```

time: 397 us -> 187 us (0.47)
  the two profiles are of different devices: /device:TPU:15 before, /device:TPU:127 now
where the time goes in v3:
time: 187 us
  Pallas kernels  176 us (94%)
  other arithmetic  6.29 us (3%)
  local copies, waits for them, and re-layouts  4.9 us (3%)
    pallas_call x1, Pallas kernels, on_device(): pl.pallas_call(kernel, out_shape=jax.ShapeDtypeStruct((CHUNK, 8192), bf),...  176 us

profile of v3, /device:TPU:127, one launch (start us, length us, event | category | flops | bytes accessed | tf_op | source)
XLA Modules:
  0.0 186.7 jit_solution(2168577229693677410)
XLA Ops:
  0.0 0.0 copy-start
  0.0 0.7 convert_element_type.20
  0.8 0.7 slice.23
  1.5 0.8 fusion.6
  2.3 1.1 fusion.7
  3.4 1.9 %fusion.hot_hbm = bf16[2560,128]{1,0:T(8,128)(2,1)} fusion(s32[2560]{0:T(1024)S(1)} %fusion.6), kind=kLoop, calls=%fused_computation.1 | loop fusion | flops 655360 | bytes 665600 | tf_op jit(solution)/shard_map/convert_element_type | solution.py:531
  5.3 1.7 fusion.5
  7.0 0.0 copy-done
  7.0 1.1 fusion.2
  8.1 175.5 %shard_map.73 = bf16[128,8192]{1,0:T(8,128)(2,1)} custom-call(bf16[512,1024]{1,0:T(8,128)(2,1)} %q_hbm.1, bf16[512,128]{1,0:T(8,128)(2,1)} %get-tuple-element.5.k_hbm, bf16[512,128]{1,0:T(8,128)(2,1)} %v_hbm.1, f32[512,128]{1,0:T(8,128)} %get-tuple-element.7.cos_hbm, f32[512,128]{1,0:T(8,128)} %get-tuple-element.6.sin_hbm, bf16[2560,128]{1,0:T(8,128)(2,1)} %fusion.hot_hbm, ...), custom_call_target="tpu_custom_call" | custom-call | tf_op jit(solution)/shard_map/pallas_call | solution.py:536
  183.6 3.1 %copy.9 = bf16[128,8192]{1,0:T(8,128)(2,1)} copy(bf16[128,8192]{1,0:T(8,128)(2,1)} %shard_map.73) | data formatting | bytes 4194304
  (3 shorter events, 0.0 us)
Async XLA Ops:
  0.0 7.0 %copy-start = (bf16[512,128]{1,0:T(8,128)(2,1)S(1)}, bf16[512,128]{1,0:T(8,128)(2,1)}, u32[]{:S(2)}) copy-start(bf16[512,128]{1,0:T(8,128)(2,1)} %param.8) | copy-start | bytes 393220

commit v4 on v3

--- a/solution.py
+++ b/solution.py
@@ -42,7 +42,10 @@
     for p in range(4):
         for s, order in (("+", p), ("-", 3 - p)):
             t[("bs" + s, order)] = ("z" + s, rb / 4, (("tg", "b"),), 0.0)
-            t[("br" + s, order)] = ("z" + s, 1.0, (("bs" + s, order),), 2 * HOP)
+    for hop in (1, 2, 3):
+        for k in range(4 if hop < 3 else 2):
+            before = (("bs+", k), ("bs-", 3 - k)) if hop == 1 else (("b", hop - 1, k),)
+            t[("b", hop, k)] = ("z+", 1.0, before, rb / 4 / RATE)
     column = (("tg", "a"), ("ay+", 0), ("ay+", 1), ("ay-", 0), ("ay-", 1), ("ar+", 0), ("ar-", 1))
     for s in range(4):
         size = ra if s < 3 else ra / 2
@@ -50,9 +53,9 @@
         t[("az-", s)] = ("z-", size, column if s == 0 else (("az-", s - 1),), 0.0)
     for slot in "NF":
         for half in (0, 1):
-            pieces = (2 * half, 2 * half + 1)
-            kind = "bs" if slot == "N" else "br"
-            need = (("tg", "b"),) + tuple((kind + s, p) for s in "+-" for p in pieces)
+            need = (("tg", "b"),) + tuple(("b", 1 if slot == "N" else 2, k) for k in range(4))
+            if slot == "F":
+                need = need + (("b", 3, 0), ("b", 3, 1))
             t[("by+", slot, half)] = ("y+", rb / 2, need, 0.0)
             t[("by-", slot, half)] = ("y-", rb / 2, need, 0.0)
         t[("bq+", slot, 0)] = ("y+", rb / 2, (("by+", slot, 0),), 0.0)
@@ -97,7 +100,7 @@
             r = 0
         elif k in ("ay+", "ay-", "ar+", "ar-"):
             r = 2
-        elif k in ("bs+", "bs-", "br+", "br-"):
+        elif k in ("bs+", "bs-", "b"):
             r = 3
         elif k in ("az+", "az-"):
             r = 6
@@ -291,6 +294,15 @@
                 rows = pl.ds(m * CHUNK + (0 if sign > 0 else CHUNK // 2), CHUNK // 2)
             i = ((x + d + 4) % 4) * 2 + core
             return [(None, same(att.at[i, rows], ring(sign)))]
+        if kind == "b":
+            hop, k = name[1], name[2]
+            out = []
+            for sign, p in ((1, k), (-1, 3 - k)):
+                at_r = (4 - hop) % 4 if sign > 0 else hop % 4
+                n = NUMBER[("bs+" if sign > 0 else "bs-", p)]
+                ref = wb.at[(z - sign * hop + 8) % 8, p]
+                out.append((r == at_r, same(ref, ctx_of(sign, 0, 0))))
+            return out
         sign = 1 if kind[2] == "+" else -1
         if kind[:2] in ("ay", "ar"):
             half = name[1]
@@ -305,26 +317,8 @@
             zz = (z - sign * (s + (1 if incoming else 0)) + 8) % 8
             ref = wa.at[zz] if s < 3 else wa.at[zz, halves(0 if sign > 0 else 1)]
             return [(None, same(ref, ctx_of(sign, 0, 0)))]
-        if kind[:2] in ("bs", "br", "bz"):
-            p = name[1]
-            far = (4 - r) % 4 if sign > 0 else r
-            n = NUMBER[("bs" + kind[2], p)]
-            carried = p < 2 if sign > 0 else p >= 2
-            last = 1 if sign > 0 else 3
-            if not incoming:
-                zs = (z - sign * far + 8) % 8
-                if kind[:2] == "bs":
-                    cond = r == 0
-                else:
-                    cond = (r != 0) if carried else ((r != 0) & (r != last))
-                return [(cond, same(wb.at[zs, p], ctx_of(sign, 0, 0)))]
-            zs = (z - sign * ((far + 3) % 4 + 1) + 16) % 8
-            cp = same(wb.at[zs, p], ctx_of(sign, 0, 0))
-            near = (r == 3) if sign > 0 else ((r == 1) | (r == 2))
-            if kind[:2] == "bs":
-                return [(near, cp)]
-            far_end = (r != 0) & jnp.logical_not(near)
-            return [(far_end if kind[:2] == "br" else r == 0, cp)]
+        if kind in ("bs+", "bs-"):
+            return [] if incoming else [(r == 0, same(wb.at[z, name[1]], ctx_of(sign, 0, 0)))]
         which, half = name[1], name[2]
         step = (1 if kind[:2] == "bq" else 0) + (1 if incoming else 0)
         zs = slot(which, -sign * step)
@@ -342,19 +336,24 @@
         for name in names:
             if name not in got and name[0] != "att":
                 got.add(name)
+                if name[0] == "b":
+                    continue
                 if name[0] == "tg":
                     @pl.when(owner == t)
                     def _(name=name):
                         w_local[name[1]].wait()
+                if name[0] == "hop":
+                    name = ("b",) + name[1:]
                 for cond, cp in copies(name, True):
                     under(cond, cp.wait_recv)
 
     def send(name):
         need(TASKS[name][2])
-        if name[0] in ("br+", "br-"):
-            need([name])
-        if name[0] in ("by+", "by-") and name[1] == "F":
-            need([("bz+", p) for p in (0, 1)] if name[2] == 0 else [("bz-", p) for p in (2, 3)])
+        if name[0] == "b":
+            need([("hop",) + name[1:]])
+        if name[0] in ("by+", "by-"):
+            for hop in (1, 2) if name[1] == "N" else (1, 2, 3, 4):
+                need([("hop", hop, k) for k in range(4 if hop < 4 else 2)])
         for cond, cp in copies(name, False):
             under(cond, cp.start)
 

time: 187 us -> 133 us (0.71)
  the two profiles are of different devices: /device:TPU:127 before, /device:TPU:35 now
where the time goes in v4:
time: 133 us
  Pallas kernels  122 us (92%)
  other arithmetic  6.29 us (5%)
  local copies, waits for them, and re-layouts  4.9 us (4%)
    pallas_call x1, Pallas kernels, on_device(): pl.pallas_call(kernel, out_shape=jax.ShapeDtypeStruct((CHUNK, 8192), bf),...  122 us
    unnamed x3, local copies, waits for them, and re-layouts  3.1 us

profile of v4, /device:TPU:35, one launch (start us, length us, event | category | flops | bytes accessed | tf_op | source)
XLA Modules:
  0.0 132.8 jit_solution(5242486753439561630)
XLA Ops:
  0.0 0.0 copy-start
  0.0 0.7 convert_element_type.20
  0.8 0.7 slice.23
  1.5 0.8 fusion.6
  2.3 1.1 fusion.7
  3.4 1.9 %fusion.hot_hbm = bf16[2560,128]{1,0:T(8,128)(2,1)} fusion(s32[2560]{0:T(1024)S(1)} %fusion.6), kind=kLoop, calls=%fused_computation.1 | loop fusion | flops 655360 | bytes 665600 | tf_op jit(solution)/shard_map/convert_element_type | solution.py:530
  5.3 1.7 %fusion.5 = (f32[512,64]{1,0:T(8,128)S(1)}, f32[512,64]{1,0:T(8,128)S(1)}, f32[512,64]{1,0:T(8,128)S(1)}) fusion(f32[64]{0:T(128)S(1)} %multiply_power_fusion, f32[512]{0:T(512)S(1)} %bitcast.4, f32[512]{0:T(512)S(1)} %bitcast.5, pred[64]{0:T(512)(128)(4,1)S(1)} %get-tuple-element.16, f32[512]{0:T(512)S(1)} %bitcast.3, pred[64]{0:T(512)(128)(4,1)S(1)} %get-tuple-element.17), kind=kLoop, calls=%fused_computation.12 | loop fusion | flops 131072 | bytes 399744 | tf_op jit(solution)/shard_map/neg | solution.py:523
  7.0 0.0 copy-done
  7.0 1.1 fusion.2
  8.1 121.6 %shard_map.73 = bf16[128,8192]{1,0:T(8,128)(2,1)} custom-call(bf16[512,1024]{1,0:T(8,128)(2,1)} %q_hbm.1, bf16[512,128]{1,0:T(8,128)(2,1)} %get-tuple-element.5.k_hbm, bf16[512,128]{1,0:T(8,128)(2,1)} %v_hbm.1, f32[512,128]{1,0:T(8,128)} %get-tuple-element.7.cos_hbm, f32[512,128]{1,0:T(8,128)} %get-tuple-element.6.sin_hbm, bf16[2560,128]{1,0:T(8,128)(2,1)} %fusion.hot_hbm, ...), custom_call_target="tpu_custom_call" | custom-call | tf_op jit(solution)/shard_map/pallas_call | solution.py:535
  129.7 3.1 %copy.9 = bf16[128,8192]{1,0:T(8,128)(2,1)} copy(bf16[128,8192]{1,0:T(8,128)(2,1)} %shard_map.73) | data formatting | bytes 4194304
  (3 shorter events, 0.0 us)
Async XLA Ops:
  0.0 7.0 %copy-start = (bf16[512,128]{1,0:T(8,128)(2,1)S(1)}, bf16[512,128]{1,0:T(8,128)(2,1)}, u32[]{:S(2)}) copy-start(bf16[512,128]{1,0:T(8,128)(2,1)} %param.8) | copy-start | bytes 393220

commit v5 on v4

--- a/solution.py
+++ b/solution.py
@@ -16,46 +16,56 @@
 WINDOW = BACK * TOK + CHUNK
 ROWS_A = 512
 ROWS_B = 1024 - ROWS_A
-RATE = 45.5
-HOP = 1.9
-STEP = 3.0
+RATE = 43.0
+HOP = 2.0
+STEP = 2.9
 AHEAD = 6.0
 BIG = 2.0**100
 theta_base = 1000000.0
 MESH = pl.DeviceIdType.MESH
-PARTS = ((0, 1, -1, 2), (-2, 3, -3, 4))
-NEAR = (0, 1, 2, -1)
+ORDERED = (0, 1, -1, 2, -2, 3, -3, 4)
+PARTS = ((0, 4), (4, 3), (7, 1))
+DEPTH = (2, 3, 4)
 
 
 def build_tasks():
     t = {}
     ra, rb = float(ROWS_A), float(ROWS_B)
-    for j in range(1, BACK + 1):
-        t[("kv", j)] = ("y+" if j < 3 else "x+", 256.0, (), 2.0)
-    for k, rows in (("a", ra), ("b", rb)):
-        t[("tg", k)] = ("x-", rows / 4, (), 1.0)
-    for half in (0, 1):
-        t[("ay+", half)] = ("y+", ra / 4, (("tg", "a"),), 0.0)
-        t[("ay-", half)] = ("y-", ra / 4, (("tg", "a"),), 0.0)
-    t[("ar+", 0)] = ("y+", ra / 4, (("ay+", 0),), 0.0)
-    t[("ar-", 1)] = ("y-", ra / 4, (("ay-", 1),), 0.0)
+    t[("kv", 4)] = ("x+", 256.0, (), 2.0)
+    t[("tg", "b")] = ("x-", rb / 4, (), 3.0)
+    t[("tg", "a")] = ("x-", ra / 4, (), 3.0)
+    for j, link in ((1, "y+"), (3, "y-"), (2, "y+")):
+        t[("kv", j)] = (link, 128.0, (), 0.0)
+    for j, link in ((1, "y+"), (3, "y-"), (2, "y+")):
+        t[("kw", j)] = (link, 128.0, (("kv", 4),), 2.0)
+    t[("ay", 1)] = ("y+", ra / 4, (("tg", "a"),), 2.0)
+    t[("ay", -1)] = ("y-", ra / 4, (("tg", "a"),), 2.0)
+    t[("ay", 2)] = ("y+", ra / 4, (("tg", "a"),), 4.0)
     for p in range(4):
-        for s, order in (("+", p), ("-", 3 - p)):
-            t[("bs" + s, order)] = ("z" + s, rb / 4, (("tg", "b"),), 0.0)
-    for hop in (1, 2, 3):
-        for k in range(4 if hop < 3 else 2):
-            before = (("bs+", k), ("bs-", 3 - k)) if hop == 1 else (("b", hop - 1, k),)
-            t[("b", hop, k)] = ("z+", 1.0, before, rb / 4 / RATE)
-    column = (("tg", "a"), ("ay+", 0), ("ay+", 1), ("ay-", 0), ("ay-", 1), ("ar+", 0), ("ar-", 1))
+        for d in (1, -1, -2):
+            t[("bs", d, p)] = ("z+" if d > 0 else "z-", rb / 8 if d != -2 else rb / 8, (("tg", "b"),), 1.0)
+    far = {
+        1: (("bs", 1), ("bs", -2)),
+        2: (("bf", 1),),
+        3: (("bf", 2), ("bf", 1)),
+    }
+    for stage in (1, 2, 3):
+        for p in range(4):
+            t[("bf", stage, p)] = (
+                "z+", 1.0, tuple(k + (p,) for k in far[stage]), rb / 4 / RATE)
+    column = (("tg", "a"), ("ay", 1), ("ay", -1), ("ay", 2))
     for s in range(4):
         size = ra if s < 3 else ra / 2
         t[("az+", s)] = ("z+", size, column if s == 0 else (("az+", s - 1),), 0.0)
         t[("az-", s)] = ("z-", size, column if s == 0 else (("az-", s - 1),), 0.0)
     for slot in "NF":
         for half in (0, 1):
-            need = (("tg", "b"),) + tuple(("b", 1 if slot == "N" else 2, k) for k in range(4))
-            if slot == "F":
-                need = need + (("b", 3, 0), ("b", 3, 1))
+            pieces = (2 * half, 2 * half + 1)
+            need = (("tg", "b"),)
+            if slot == "N":
+                need += tuple(("bs", d, p) for d in (1, -1, -2) for p in pieces)
+            else:
+                need += tuple(("bf", stage, p) for stage in (1, 2, 3) for p in pieces)
             t[("by+", slot, half)] = ("y+", rb / 2, need, 0.0)
             t[("by-", slot, half)] = ("y-", rb / 2, need, 0.0)
         t[("bq+", slot, 0)] = ("y+", rb / 2, (("by+", slot, 0),), 0.0)
@@ -84,8 +94,7 @@
     need = [("am", m, k) for k in ("own", "+", "-", "+2", "-2")]
     need += [("at+", m), ("at-", m), ("ar2+", m), ("ar2-", m)]
     need += b_names("N" if part == 0 else "NF")
-    deep = 2 if part == 0 else 4
-    for s in range(deep):
+    for s in range(DEPTH[part]):
         need += [("az+", s), ("az-", s)]
     return tuple(need)
 
@@ -95,12 +104,16 @@
     for n, name in enumerate(t):
         k = name[0]
         if k == "kv":
-            r = 1
+            r = 0
+        elif k == "kw":
+            r = 0.55
         elif k == "tg":
             r = 0
-        elif k in ("ay+", "ay-", "ar+", "ar-"):
-            r = 2
-        elif k in ("bs+", "bs-", "b"):
+        elif k == "ay":
+            r = 0.6
+        elif k == "bs":
+            r = 0.5
+        elif k == "bf":
             r = 3
         elif k in ("az+", "az-"):
             r = 6
@@ -117,9 +130,9 @@
     pending = sorted(t, key=lambda k: rank[k])
     order, now = [], 0.0
     steps = [(m, g) for m in range(4) for g in range(2)]
-    mats = [(m, part) for part in range(2) for m in range(4)]
+    mats = [(m, part) for part in range(len(PARTS)) for m in range(4)]
     finals = []
-    sent = {0: [], 1: []}
+    sent = {part: [] for part in range(len(PARTS))}
 
     def ready(names):
         return all(arrive.get(n, 1e9) <= now for n in names)
@@ -131,12 +144,14 @@
 
     while pending or steps or mats or finals:
         for n in list(pending):
+            if len(steps) == 8 and n[0] not in ("tg", "kv", "kw", "ay", "bs"):
+                continue
             if ready(t[n][2]) and link_free.get(t[n][0], 0.0) - now < AHEAD:
                 order.append(("send", n))
                 send(n, *[t[n][i] for i in (0, 1, 3)])
                 pending.remove(n)
         if steps:
-            if ready([("kv", j) for j in range(1, BACK + 1)]):
+            if ready([("kv", j) for j in range(1, BACK + 1)] + [("kw", j) for j in (1, 2, 3)]):
                 m, g = steps.pop(0)
                 order.append(("step", m, g))
                 now += STEP
@@ -149,8 +164,8 @@
                 m, part = ok[0]
                 mats.remove(ok[0])
                 order.append(("M", m, part))
-                now += 1.5
-                send(("c", m, part), "x+", 140.0, 1.0)
+                now += 0.35 * PARTS[part][1]
+                send(("c", m, part), "x+", 35.0 * PARTS[part][1], 1.0)
                 sent[part].append(("c", m, part))
                 if len(sent[part]) == 4:
                     finals.append(part)
@@ -196,16 +211,15 @@
 
     mate = (c, chip * 2 + (1 - core))
     barrier = pltpu.get_barrier_semaphore()
-    partners = [ctx_of(1, 0, 0), ctx_of(-1, 0, 0), ctx_of(0, 0, 1), ctx_of(0, 0, -1)]
+    partners = [ctx_of(1, 0, 0), ctx_of(-1, 0, 0), ctx_of(0, 0, 1), ctx_of(0, 0, -1), ctx_of(0, 0, 2), ctx_of(2, 0, 0), ctx_of(-2, 0, 0)]
     for d in range(4):
         for k in range(2):
             other = (x + d) % 4
             who = (z * 8 + (other // 2) * 4 + y, (other % 2) * 2 + (core + k) % 2)
             if d or k:
                 partners.append(who)
-    for j in range(1, BACK + 1):
+    for j in (BACK, 64 - BACK):
         partners.append(((c + j) % 64, t))
-        partners.append(((c - j + 64) % 64, t))
     for d in partners:
         pl.semaphore_signal(barrier, inc=1, device_id=d, device_id_type=MESH)
 
@@ -261,12 +275,20 @@
         def same(ref, dev, **k):
             return one(ref, ref, dev, **k)
 
-        if kind == "kv":
+        if kind in ("kv", "kw"):
             j = name[1]
-            dev = ((c + j) % 64, t)
             to = pl.ds((BACK - j) * TOK, TOK)
-            return [(None, one(kbuf.at[own], kbuf.at[to], dev)),
-                    (None, one(vbuf.at[own], vbuf.at[to], dev, kv_send.at[j - 1], kv_recv.at[j - 1]))]
+            n = NUMBER[("kv", j)]
+            wrap = y + j >= 4
+            dev = ((c + 4) % 64, t) if j == 4 else ctx_of(0, 0, j)
+            cond = None if j == 4 else (wrap if kind == "kw" else jnp.logical_not(wrap))
+            at = own if kind == "kv" else pl.ds(0, TOK)
+            if incoming:
+                if kind == "kw":
+                    return []
+                cond = None
+            return [(cond, one(kbuf.at[at], kbuf.at[to], dev)),
+                    (cond, one(vbuf.at[at], vbuf.at[to], dev, kv_send.at[j - 1], kv_recv.at[j - 1]))]
         if kind == "tg":
             k = name[1]
             i = "ab".index(k)
@@ -294,31 +316,35 @@
                 rows = pl.ds(m * CHUNK + (0 if sign > 0 else CHUNK // 2), CHUNK // 2)
             i = ((x + d + 4) % 4) * 2 + core
             return [(None, same(att.at[i, rows], ring(sign)))]
-        if kind == "b":
-            hop, k = name[1], name[2]
+        if kind == "ay":
+            d = name[1]
+            cond = (r == (4 - d) % 4) if incoming else (r == 0)
+            return [(cond, same(wa.at[z], ctx_of(0, 0, d)))]
+        if kind == "bs":
+            d, p = name[1], name[2]
+            zs = (z - (d if incoming else 0) + 8) % 8
+            cond = (r == (4 - d) % 4) if incoming else (r == 0)
+            return [(cond, same(wb.at[zs, p], ctx_of(d, 0, 0)))]
+        if kind == "bf":
+            stage, p = name[1], name[2]
             out = []
-            for sign, p in ((1, k), (-1, 3 - k)):
-                at_r = (4 - hop) % 4 if sign > 0 else hop % 4
-                n = NUMBER[("bs+" if sign > 0 else "bs-", p)]
-                ref = wb.at[(z - sign * hop + 8) % 8, p]
-                out.append((r == at_r, same(ref, ctx_of(sign, 0, 0))))
+            for sign, sender, carried in {
+                1: ((1, 3, 1), (-1, 2, 2)),
+                2: ((1, 2, 2),),
+                3: ((1, 1, 3), (-1, 3, 3)),
+            }[stage]:
+                if stage == 3 and (p < 2) != (sign > 0):
+                    continue
+                rr = (sender - sign + 4) % 4 if incoming else sender
+                zs = (z - sign * (carried + (1 if incoming else 0)) + 8) % 8
+                out.append((r == rr, same(wb.at[zs, p], ctx_of(sign, 0, 0))))
             return out
         sign = 1 if kind[2] == "+" else -1
-        if kind[:2] in ("ay", "ar"):
-            half = name[1]
-            ref = wa.at[z, halves(half)]
-            if kind[:2] == "ay":
-                cond = (r == (3 if sign > 0 else 1)) if incoming else (r == 0)
-            else:
-                cond = (r == 2) if incoming else (r == (3 if sign > 0 else 1))
-            return [(cond, same(ref, ctx_of(0, 0, sign)))]
         if kind[:2] == "az":
             s = name[1]
             zz = (z - sign * (s + (1 if incoming else 0)) + 8) % 8
             ref = wa.at[zz] if s < 3 else wa.at[zz, halves(0 if sign > 0 else 1)]
             return [(None, same(ref, ctx_of(sign, 0, 0)))]
-        if kind in ("bs+", "bs-"):
-            return [] if incoming else [(r == 0, same(wb.at[z, name[1]], ctx_of(sign, 0, 0)))]
         which, half = name[1], name[2]
         step = (1 if kind[:2] == "bq" else 0) + (1 if incoming else 0)
         zs = slot(which, -sign * step)
@@ -336,24 +362,15 @@
         for name in names:
             if name not in got and name[0] != "att":
                 got.add(name)
-                if name[0] == "b":
-                    continue
                 if name[0] == "tg":
                     @pl.when(owner == t)
                     def _(name=name):
                         w_local[name[1]].wait()
-                if name[0] == "hop":
-                    name = ("b",) + name[1:]
                 for cond, cp in copies(name, True):
                     under(cond, cp.wait_recv)
 
     def send(name):
         need(TASKS[name][2])
-        if name[0] == "b":
-            need([("hop",) + name[1:]])
-        if name[0] in ("by+", "by-"):
-            for hop in (1, 2) if name[1] == "N" else (1, 2, 3, 4):
-                need([("hop", hop, k) for k in range(4 if hop < 4 else 2)])
         for cond, cp in copies(name, False):
             under(cond, cp.start)
 
@@ -398,35 +415,39 @@
             att[me, rows, pl.ds(pl.multiple_of((g * 4 + i) * HD, HD), HD)] = (
                 result[i * CHUNK:(i + 1) * CHUNK])
 
+    def part_cols(part):
+        return pl.ds(PARTS[part][0] * HD, PARTS[part][1] * HD)
+
     def c_copy(m, hh, part):
         return pltpu.make_async_remote_copy(
-            src_ref=csend.at[m, hh, part], dst_ref=crecv.at[me, part],
+            src_ref=csend.at[m, hh, :, part_cols(part)], dst_ref=crecv.at[me, :, part_cols(part)],
             send_sem=c_send.at[m, hh, part], recv_sem=c_recv.at[me, part],
             device_id=(z * 8 + hh * 4 + y, m), device_id_type=MESH)
 
     def matmul(m, part):
         need(mat_needs(m, part))
         rows = pl.ds(m * CHUNK, CHUNK)
-        for pair in range(2):
+        begin, count = PARTS[part]
+        for at in range(begin, begin + count, 2):
             total = None
-            z0, z1 = [(z + PARTS[part][2 * pair + i] + 8) % 8 for i in range(2)]
+            wide = range(at, min(at + 2, begin + count))
+            zs = [(z + ORDERED[i] + 8) % 8 for i in wide]
             for u in range(4):
                 lhs = jnp.concatenate([att[u, rows, :], att[4 + u, rows, :]], axis=0)
-                rhs = jnp.concatenate(
-                    [jnp.concatenate([wa[z0, u], wb[z0, u]], axis=0),
-                     jnp.concatenate([wa[z1, u], wb[z1, u]], axis=0)], axis=1)
+                rhs = [jnp.concatenate([wa[i, u], wb[i, u]], axis=0) for i in zs]
+                rhs = jnp.concatenate(rhs, axis=1) if len(rhs) > 1 else rhs[0]
                 one = jnp.dot(lhs, rhs, preferred_element_type=jnp.float32)
                 total = one if total is None else total + one
             total = total.astype(jnp.bfloat16)
-            cols = pl.ds(pair * 256, 256)
+            cols = pl.ds(at * HD, len(wide) * HD)
             for hh in range(2):
-                csend[m, hh, part, :, cols] = total[hh * CHUNK:(hh + 1) * CHUNK]
+                csend[m, hh, :, cols] = total[hh * CHUNK:(hh + 1) * CHUNK]
         for hh in range(2):
             mine = (h == hh) & (t == m)
 
             @pl.when(mine)
             def _(hh=hh):
-                crecv[me, part] = csend[m, hh, part]
+                crecv[me, :, part_cols(part)] = csend[m, hh, :, part_cols(part)]
 
             pl.when(jnp.logical_not(mine))(c_copy(m, hh, part).start)
 
@@ -437,15 +458,15 @@
         def body(s, carry):
             hs, ts = s // 4, s % 4
             cp = pltpu.make_async_remote_copy(
-                src_ref=csend.at[0, 0, part], dst_ref=crecv.at[s, part],
+                src_ref=csend.at[0, 0, :, part_cols(part)], dst_ref=crecv.at[s, :, part_cols(part)],
                 send_sem=c_send.at[0, 0, part], recv_sem=c_recv.at[s, part],
                 device_id=mate, device_id_type=MESH)
             pl.when(s != me)(cp.wait_recv)
-            for i, dz in enumerate(PARTS[part]):
-                zs = (z + dz + 8) % 8
+            for i in range(PARTS[part][0], sum(PARTS[part])):
+                zs = (z + ORDERED[i] + 8) % 8
                 col = (zs * 8 + hs * 4 + (ts - zs + 8) % 4) * HD
                 wide = pl.ds(pl.multiple_of(col, HD), HD)
-                got_c = crecv[s, part, :, i * HD:(i + 1) * HD].astype(jnp.float32)
+                got_c = crecv[s, :, i * HD:(i + 1) * HD].astype(jnp.float32)
                 out_ref[:, wide] = (got_c + res[:, wide].astype(jnp.float32)).astype(jnp.bfloat16)
             return carry
 
@@ -456,7 +477,7 @@
     last = max(i for i, it in enumerate(items) if it[0] == "step")
     rotated = False
     for it in items[:first]:
-        if not rotated and it[1][0] not in ("tg", "kv"):
+        if not rotated and it[1][0] != "tg" and it[1][0] != "kv":
             rotated = True
             with jax.named_scope("rotq"):
                 rotate_queries()
@@ -497,7 +518,7 @@
             under(cond, cp.wait_send)
     for m in range(4):
         for hh in range(2):
-            for part in range(2):
+            for part in range(len(PARTS)):
                 pl.when(jnp.logical_not((h == hh) & (t == m)))(c_copy(m, hh, part).wait_send)
 
 
@@ -547,16 +568,16 @@
             pltpu.VMEM((SPAN, HD), bf),
             pltpu.VMEM((SPAN, HD), bf),
             pltpu.VMEM((8, TOK, 1024), bf),
-            pltpu.VMEM((4, 2, 2, CHUNK, 512), bf),
-            pltpu.VMEM((8, 2, CHUNK, 512), bf),
+            pltpu.VMEM((4, 2, CHUNK, 1024), bf),
+            pltpu.VMEM((8, CHUNK, 1024), bf),
             pltpu.VMEM((CHUNK, 8192), bf),
             dma((nt,)),
             dma((nt,)),
             dma((BACK,)),
             dma((BACK,)),
             dma((2, 4)),
-            dma((4, 2, 2)),
-            dma((8, 2)),
+            dma((4, 2, len(PARTS))),
+            dma((8, len(PARTS))),
             dma((9,)),
         ],
         compiler_params=pltpu.CompilerParams(

time: 133 us -> 123 us (0.925)
  the two profiles are of different devices: /device:TPU:35 before, /device:TPU:15 now
where the time goes in v5:
time: 123 us; the launch traced here: 121 us
  Pallas kernels  110 us (89%)
  other arithmetic  6.29 us (5%)
  local copies, waits for them, and re-layouts  4.9 us (4%)
    pallas_call x1, Pallas kernels, on_device(): pl.pallas_call(kernel, out_shape=jax.ShapeDtypeStruct((CHUNK, 8192), bf),...  110 us
    unnamed x3, local copies, waits for them, and re-layouts  3.1 us

profile of v5, /device:TPU:15, one launch (start us, length us, event | category | flops | bytes accessed | tf_op | source)
XLA Modules:
  0.0 121.2 jit_solution(12886586181675820883)
XLA Ops:
  0.0 0.0 copy-start
  0.0 0.7 convert_element_type.20
  0.8 0.7 slice.23
  1.5 0.8 fusion.6
  2.3 1.1 fusion.7
  3.4 1.9 %fusion.hot_hbm = bf16[2560,128]{1,0:T(8,128)(2,1)} fusion(s32[2560]{0:T(1024)S(1)} %fusion.6), kind=kLoop, calls=%fused_computation.1 | loop fusion | flops 655360 | bytes 665600 | tf_op jit(solution)/shard_map/convert_element_type | solution.py:551
  5.3 1.7 %fusion.5 = (f32[512,64]{1,0:T(8,128)S(1)}, f32[512,64]{1,0:T(8,128)S(1)}, f32[512,64]{1,0:T(8,128)S(1)}) fusion(f32[64]{0:T(128)S(1)} %multiply_power_fusion, f32[512]{0:T(512)S(1)} %bitcast.4, f32[512]{0:T(512)S(1)} %bitcast.5, pred[64]{0:T(512)(128)(4,1)S(1)} %get-tuple-element.16, f32[512]{0:T(512)S(1)} %bitcast.3, pred[64]{0:T(512)(128)(4,1)S(1)} %get-tuple-element.17), kind=kLoop, calls=%fused_computation.12 | loop fusion | flops 131072 | bytes 399744 | tf_op jit(solution)/shard_map/neg | solution.py:544
  7.0 0.0 copy-done
  7.0 1.1 fusion.2
  8.1 110.0 %shard_map.73 = bf16[128,8192]{1,0:T(8,128)(2,1)} custom-call(bf16[512,1024]{1,0:T(8,128)(2,1)} %q_hbm.1, bf16[512,128]{1,0:T(8,128)(2,1)} %get-tuple-element.5.k_hbm, bf16[512,128]{1,0:T(8,128)(2,1)} %v_hbm.1, f32[512,128]{1,0:T(8,128)} %get-tuple-element.7.cos_hbm, f32[512,128]{1,0:T(8,128)} %get-tuple-element.6.sin_hbm, bf16[2560,128]{1,0:T(8,128)(2,1)} %fusion.hot_hbm, ...), custom_call_target="tpu_custom_call" | custom-call | tf_op jit(solution)/shard_map/pallas_call | solution.py:556
  118.1 3.1 %copy.9 = bf16[128,8192]{1,0:T(8,128)(2,1)} copy(bf16[128,8192]{1,0:T(8,128)(2,1)} %shard_map.73) | data formatting | bytes 4194304
  (3 shorter events, 0.0 us)
Async XLA Ops:
  0.0 7.0 %copy-start = (bf16[512,128]{1,0:T(8,128)(2,1)S(1)}, bf16[512,128]{1,0:T(8,128)(2,1)}, u32[]{:S(2)}) copy-start(bf16[512,128]{1,0:T(8,128)(2,1)} %param.8) | copy-start | bytes 393220

commit v6 on v5

--- a/solution.py
+++ b/solution.py
@@ -14,7 +14,7 @@
 BACK = 4
 SPAN = (BACK + 1) * TOK
 WINDOW = BACK * TOK + CHUNK
-ROWS_A = 512
+ROWS_A = 384
 ROWS_B = 1024 - ROWS_A
 RATE = 43.0
 HOP = 2.0
@@ -38,9 +38,9 @@
         t[("kv", j)] = (link, 128.0, (), 0.0)
     for j, link in ((1, "y+"), (3, "y-"), (2, "y+")):
         t[("kw", j)] = (link, 128.0, (("kv", 4),), 2.0)
-    t[("ay", 1)] = ("y+", ra / 4, (("tg", "a"),), 2.0)
-    t[("ay", -1)] = ("y-", ra / 4, (("tg", "a"),), 2.0)
-    t[("ay", 2)] = ("y+", ra / 4, (("tg", "a"),), 4.0)
+    t[("ay", 1)] = ("y+", ra / 4, (("tg", "a"),), 10.0)
+    t[("ay", -1)] = ("y-", ra / 4, (("tg", "a"),), 10.0)
+    t[("ay", 2)] = ("y+", ra / 4, (("tg", "a"),), 10.0)
     for p in range(4):
         for d in (1, -1, -2):
             t[("bs", d, p)] = ("z+" if d > 0 else "z-", rb / 8 if d != -2 else rb / 8, (("tg", "b"),), 1.0)
@@ -187,9 +187,26 @@
 NUMBER = {n: i for i, n in enumerate(NAMES)}
 
 
+def cos_sin(angle):
+    turns = jnp.floor(angle * (2.0 / math.pi) + 0.5)
+    a = angle - turns * 1.5703125
+    a = a - turns * 4.837512969970703125e-4
+    a = a - turns * 7.549789948768648e-8
+    quarter = turns - 4.0 * jnp.floor(turns * 0.25)
+    s = a * a
+    sine = a + a * s * (-1.6666654611e-1 + s * (8.3321608736e-3 - s * 1.9515295891e-4))
+    cosine = 1.0 - 0.5 * s + s * s * (
+        4.166664568298827e-2 + s * (-1.388731625493765e-3 + s * 2.443315711809948e-5))
+    odd = (quarter == 1.0) | (quarter == 3.0)
+    low_c = (quarter == 1.0) | (quarter == 2.0)
+    c = jnp.where(odd, sine, cosine)
+    d = jnp.where(odd, cosine, sine)
+    return jnp.where(low_c, -c, c), jnp.where(quarter >= 2.0, -d, d)
+
+
 def kernel(
-    q_hbm, k_hbm, v_hbm, cos_hbm, sin_hbm, hot_hbm, w_hbm, res_hbm, out_ref,
-    wa, wb, q, cos, sin, kbuf, vbuf, hot, att, csend, crecv, res,
+    q_hbm, k_hbm, v_hbm, pos_hbm, seg_hbm, freq_ref, w_hbm, res_hbm, out_ref,
+    wa, wb, q, cos, sin, kraw, kbuf, vbuf, hot, pos, seg, att, csend, crecv, res,
     send_sem, recv_sem, kv_send, kv_recv, tg_recv, c_send, c_recv, local,
 ):
     c = lax.axis_index("ctx")
@@ -225,12 +242,11 @@
 
     own = pl.ds(BACK * TOK, TOK)
     loads = {
-        "k": pltpu.make_async_copy(k_hbm, kbuf.at[own], local.at[0]),
+        "pos": pltpu.make_async_copy(pos_hbm, pos.at[pl.ds(0, 3)], local.at[3]),
+        "k": pltpu.make_async_copy(k_hbm, kraw, local.at[0]),
+        "seg": pltpu.make_async_copy(seg_hbm, seg, local.at[4]),
         "v": pltpu.make_async_copy(v_hbm, vbuf.at[own], local.at[1]),
         "q": pltpu.make_async_copy(q_hbm, q, local.at[2]),
-        "cos": pltpu.make_async_copy(cos_hbm, cos, local.at[3]),
-        "sin": pltpu.make_async_copy(sin_hbm, sin, local.at[4]),
-        "hot": pltpu.make_async_copy(hot_hbm, hot, local.at[5]),
         "res": pltpu.make_async_copy(res_hbm, res, local.at[6]),
     }
     for cp in loads.values():
@@ -247,11 +263,32 @@
         for k in "ab":
             w_local[k].start()
 
+    with jax.named_scope("tables"):
+        pos[3:8, :] = jnp.zeros((5, TOK), jnp.int32)
+        loads["pos"].wait()
+        place = jnp.transpose(pos[...].astype(jnp.float32))
+        lane = lax.broadcasted_iota(jnp.int32, (TOK, HD), 1) % (HD // 2)
+        chosen = jnp.where(
+            lane < HD // 8, place[:, 0:1],
+            jnp.where(lane < HD // 8 + 3 * HD // 16, place[:, 1:2], place[:, 2:3]))
+        cosine, sine = cos_sin(chosen * freq_ref[0:1, :])
+        upper = lax.broadcasted_iota(jnp.int32, (TOK, HD), 1) < HD // 2
+        cos[...] = cosine
+        sin[...] = jnp.where(upper, -sine, sine)
+        loads["k"].wait()
+        kf = kraw[...].astype(jnp.float32)
+        kbuf[own, :] = (kf * cos[...] + pltpu.roll(kf, HD // 2, 1) * sin[...]).astype(jnp.bfloat16)
+        loads["v"].wait()
+        loads["seg"].wait()
+        for j in range(BACK + 1):
+            rows = seg[pl.ds(((c - BACK + j + 64) % 64) * 4, 4), :].astype(jnp.float32)
+            turned = jnp.transpose(jnp.concatenate([rows, rows], axis=0))
+            ids = lax.broadcasted_iota(jnp.int32, (HD, HD), 1).astype(jnp.float32)
+            for i in range(4):
+                hot[pl.ds(j * TOK + i * HD, HD), :] = (
+                    turned[:, i:i + 1] == ids).astype(jnp.float32).astype(jnp.bfloat16)
     with jax.named_scope("barrier"):
         pl.semaphore_wait(barrier, len(partners))
-    with jax.named_scope("kvload"):
-        loads["k"].wait()
-        loads["v"].wait()
 
     def slot(which, dy):
         rr = (r - dy + 8) % 4
@@ -287,8 +324,8 @@
                 if kind == "kw":
                     return []
                 cond = None
-            return [(cond, one(kbuf.at[at], kbuf.at[to], dev)),
-                    (cond, one(vbuf.at[at], vbuf.at[to], dev, kv_send.at[j - 1], kv_recv.at[j - 1]))]
+            return [(cond, one(vbuf.at[at], vbuf.at[to], dev, kv_send.at[j - 1], kv_recv.at[j - 1])),
+                    (cond, one(kbuf.at[at], kbuf.at[to], dev))]
         if kind == "tg":
             k = name[1]
             i = "ab".index(k)
@@ -377,8 +414,7 @@
     scale2 = (1.0 / math.sqrt(HD)) * math.log2(math.e)
 
     def rotate_queries():
-        for k in ("q", "cos", "sin", "hot"):
-            loads[k].wait()
+        loads["q"].wait()
 
         def body(hd, carry):
             cols = pl.ds(pl.multiple_of(hd * HD, HD), HD)
@@ -522,33 +558,10 @@
                 pl.when(jnp.logical_not((h == hh) & (t == m)))(c_copy(m, hh, part).wait_send)
 
 
-def rotary_tables(positions):
-    half_dim = HD // 2
-    freq_index = jnp.arange(half_dim)
-    inv_freq = theta_base ** (-2.0 * freq_index.astype(jnp.float32) / HD)
-    first_end = HD // 8
-    second_end = first_end + 3 * HD // 16
-    place = positions.astype(jnp.float32)
-    chosen = jnp.where(
-        freq_index[None, :] < first_end,
-        place[0][:, None],
-        jnp.where(freq_index[None, :] < second_end, place[1][:, None], place[2][:, None]),
-    )
-    angle = chosen * inv_freq[None, :]
-    return (jnp.cos(angle), jnp.sin(angle))
-
-
 def on_device(queries, keys, values, positions, segment_ids, out_weight, residual):
-    cosine, sine = rotary_tables(positions)
-    cos2 = jnp.concatenate([cosine, cosine], axis=1)
-    sin2 = jnp.concatenate([-sine, sine], axis=1)
-    kf = keys.astype(jnp.float32)
-    swapped = jnp.concatenate([kf[:, HD // 2:], kf[:, :HD // 2]], axis=1)
-    rot_k = (kf * cos2 + swapped * sin2).astype(jnp.bfloat16)
-    my = lax.axis_index("ctx")
-    wrapped = jnp.concatenate([segment_ids[-BACK * TOK:], segment_ids])
-    window = lax.dynamic_slice_in_dim(wrapped, my * TOK, SPAN, 0)
-    hot = (window[:, None] == jnp.arange(HD, dtype=jnp.int32)[None, :]).astype(jnp.bfloat16)
+    half = jnp.arange(HD // 2).astype(jnp.float32)
+    freq = theta_base ** (-2.0 * half / HD)
+    freq = jnp.broadcast_to(jnp.concatenate([freq, freq])[None], (8, HD))
     anyspec = pl.BlockSpec(memory_space=pl.ANY)
     nt = len(NAMES)
     bf, f32 = jnp.bfloat16, jnp.float32
@@ -556,7 +569,7 @@
     return pl.pallas_call(
         kernel,
         out_shape=jax.ShapeDtypeStruct((CHUNK, 8192), bf),
-        in_specs=[anyspec] * 8,
+        in_specs=[anyspec] * 5 + [pl.BlockSpec(memory_space=pltpu.VMEM)] + [anyspec] * 2,
         out_specs=pl.BlockSpec(memory_space=pltpu.VMEM),
         scratch_shapes=[
             pltpu.VMEM((8, 4, ROWS_A, HD), bf),
@@ -564,9 +577,12 @@
             pltpu.VMEM((TOK, 1024), bf),
             pltpu.VMEM((TOK, HD), f32),
             pltpu.VMEM((TOK, HD), f32),
+            pltpu.VMEM((TOK, HD), bf),
             pltpu.VMEM((SPAN, HD), bf),
             pltpu.VMEM((SPAN, HD), bf),
             pltpu.VMEM((SPAN, HD), bf),
+            pltpu.VMEM((8, TOK), jnp.int32),
+            pltpu.VMEM((256, HD), jnp.int32),
             pltpu.VMEM((8, TOK, 1024), bf),
             pltpu.VMEM((4, 2, CHUNK, 1024), bf),
             pltpu.VMEM((8, CHUNK, 1024), bf),
@@ -582,7 +598,7 @@
         ],
         compiler_params=pltpu.CompilerParams(
             collective_id=0, has_side_effects=True, vmem_limit_bytes=62 * 1024 * 1024),
-    )(queries, rot_k, values, cos2, sin2, hot, out_weight, residual)
+    )(queries, keys, values, positions, segment_ids.reshape(256, HD), freq, out_weight, residual)
 
 
 def solution(mesh):

time: 123 us -> 114 us (0.927); the launches traced: 121 us -> 114 us
  other arithmetic: 6.29 us -> 0.08 us
    convert_element_type x3 -> x0, other arithmetic: 3.77 us -> none  [the longest x1 1.9 us: on_device(): (window[:, None] == jnp.arange(HD, dtype=jnp.int32)[None, :]).astype(jnp....]
    slice x3 -> x0, local copies, waits for them, and re-layouts: 1.8 us -> none  [the longest x1 1.09 us: on_device(): swapped = jnp.concatenate([kf[:, HD // 2:], kf[:, :HD // 2]], axis=1)]
    neg x1 -> x0, other arithmetic: 1.71 us -> none  [on_device(): sin2 = jnp.concatenate([-sine, sine], axis=1)]
    unnamed x3 -> x1, local copies, waits for them, and re-layouts: 3.1 us -> 3.1 us
where the time goes in v6:
time: 114 us
  Pallas kernels  110 us (96%)
  local copies, waits for them, and re-layouts  3.7 us (3%)
    pallas_call x1, Pallas kernels, on_device(): pl.pallas_call(kernel, out_shape=jax.ShapeDtypeStruct((CHUNK, 8192), bf),...  110 us
    unnamed x1, local copies, waits for them, and re-layouts  3.1 us

profile of v6, /device:TPU:15, one launch (start us, length us, event | category | flops | bytes accessed | tf_op | source)
XLA Modules:
  0.0 113.9 jit_solution(18438723283217466282)
XLA Ops:
  0.0 0.1 pad_maximum_fusion
  0.1 0.6 broadcast_in_dim.2.freq_ref
  0.7 110.1 %shard_map.73 = bf16[128,8192]{1,0:T(8,128)(2,1)} custom-call(bf16[512,1024]{1,0:T(8,128)(2,1)} %q_hbm.1, bf16[512,128]{1,0:T(8,128)(2,1)} %k_hbm.1, bf16[512,128]{1,0:T(8,128)(2,1)} %v_hbm.1, s32[3,512]{1,0:T(4,128)} %pos_hbm.1, s32[256,128]{1,0:T(8,128)} %bitcast.1, f32[8,128]{1,0:T(8,128)} %broadcast_in_dim.2.freq_ref, bf16[1024,128]{1,0:T(8,128)(2,1)} %w_hbm.1, ...), custom_call_target="tpu_custom_call" | custom-call | tf_op jit(solution)/shard_map/pallas_call | solution.py:569
  110.8 3.1 %copy.9 = bf16[128,8192]{1,0:T(8,128)(2,1)} copy(bf16[128,8192]{1,0:T(8,128)(2,1)} %shard_map.73) | data formatting | bytes 4194304
  (1 shorter events, 0.0 us)

commit v7 on v6

--- a/solution.py
+++ b/solution.py
@@ -34,9 +34,9 @@
     t[("kv", 4)] = ("x+", 256.0, (), 2.0)
     t[("tg", "b")] = ("x-", rb / 4, (), 3.0)
     t[("tg", "a")] = ("x-", ra / 4, (), 3.0)
-    for j, link in ((1, "y+"), (3, "y-"), (2, "y+")):
+    for j, link in ((2, "y-"), (1, "y+"), (3, "y-")):
         t[("kv", j)] = (link, 128.0, (), 0.0)
-    for j, link in ((1, "y+"), (3, "y-"), (2, "y+")):
+    for j, link in ((2, "y-"), (1, "y+"), (3, "y-")):
         t[("kw", j)] = (link, 128.0, (("kv", 4),), 2.0)
     t[("ay", 1)] = ("y+", ra / 4, (("tg", "a"),), 10.0)
     t[("ay", -1)] = ("y-", ra / 4, (("tg", "a"),), 10.0)
@@ -183,6 +183,29 @@
 
 TASKS = build_tasks()
 ORDER, MODEL_US, ARRIVE = plan(TASKS)
+
+
+def tail_order(head):
+    both = lambda kind, *rest: [("send", (kind + s,) + rest) for s in "+-"]
+    got = lambda m, far: [("send", ("am", m, s + far)) for s in "+-"]
+    out = both("at", 3) + [("send", ("am", 3, "own"))] + both("ar2", 1)
+    out += [("send", ("bf", 3, p)) for p in (2, 3)] + both("by", "F", 0)
+    out += got(0, "2") + both("by", "F", 1) + both("ar2", 2) + got(2, "") + both("az", 1)
+    out += got(1, "2") + [("send", ("bq+", "F", 0))] + both("ar2", 3) + got(3, "")
+    out += both("az", 2) + [("M", 0, 0)] + got(2, "2") + [("M", 1, 0), ("send", ("bq-", "F", 1))]
+    out += got(3, "2") + [("M", 2, 0)] + both("az", 3) + [("M", 3, 0)]
+    out += [("M", m, part) for part in (1, 2) for m in range(4)]
+    out += [("F", part) for part in range(3)]
+    rest = [o for o in ORDER if o not in head and o not in out]
+    assert not rest, rest
+    return [o for o in out if o not in head]
+
+
+LAST = max(i for i, o in enumerate(ORDER) if o[0] == "step")
+LATE = [("send", n) for n in (("by+", "F", 0), ("bf", 3, 2), ("bf", 3, 3))]
+HEAD = [o for o in ORDER[:LAST] if o not in LATE]
+HEAD += [("send", ("ar2+", 1)), ("send", ("ar2-", 1)), ORDER[LAST]]
+ORDER = HEAD + tail_order(HEAD)
 NAMES = list(TASKS)
 NUMBER = {n: i for i, n in enumerate(NAMES)}
 

time: 114 us -> 112 us (0.982)
  Pallas kernels: 110 us -> 108 us
    pallas_call x1, Pallas kernels: 110 us -> 108 us  [on_device(): pl.pallas_call(kernel, out_shape=jax.ShapeDtypeStruct((CHUNK, 8192), bf),...]
where the time goes in v7:
time: 112 us
  Pallas kernels  108 us (96%)
  local copies, waits for them, and re-layouts  3.7 us (3%)
    pallas_call x1, Pallas kernels, on_device(): pl.pallas_call(kernel, out_shape=jax.ShapeDtypeStruct((CHUNK, 8192), bf),...  108 us
    unnamed x1, local copies, waits for them, and re-layouts  3.1 us

profile of v7, /device:TPU:15, one launch (start us, length us, event | category | flops | bytes accessed | tf_op | source)
XLA Modules:
  0.0 111.5 jit_solution(11033213975195708868)
XLA Ops:
  0.0 0.1 pad_maximum_fusion
  0.1 0.6 broadcast_in_dim.2.freq_ref
  0.7 107.7 %shard_map.73 = bf16[128,8192]{1,0:T(8,128)(2,1)} custom-call(bf16[512,1024]{1,0:T(8,128)(2,1)} %q_hbm.1, bf16[512,128]{1,0:T(8,128)(2,1)} %k_hbm.1, bf16[512,128]{1,0:T(8,128)(2,1)} %v_hbm.1, s32[3,512]{1,0:T(4,128)} %pos_hbm.1, s32[256,128]{1,0:T(8,128)} %bitcast.1, f32[8,128]{1,0:T(8,128)} %broadcast_in_dim.2.freq_ref, bf16[1024,128]{1,0:T(8,128)(2,1)} %w_hbm.1, ...), custom_call_target="tpu_custom_call" | custom-call | tf_op jit(solution)/shard_map/pallas_call | solution.py:592
  108.4 3.1 %copy.9 = bf16[128,8192]{1,0:T(8,128)(2,1)} copy(bf16[128,8192]{1,0:T(8,128)(2,1)} %shard_map.73) | data formatting | bytes 4194304
  (1 shorter events, 0.0 us)

commit v8 on v7

--- a/solution.py
+++ b/solution.py
@@ -14,7 +14,7 @@
 BACK = 4
 SPAN = (BACK + 1) * TOK
 WINDOW = BACK * TOK + CHUNK
-ROWS_A = 384
+ROWS_A = 352
 ROWS_B = 1024 - ROWS_A
 RATE = 43.0
 HOP = 2.0
@@ -30,7 +30,7 @@
 
 def build_tasks():
     t = {}
-    ra, rb = float(ROWS_A), float(ROWS_B)
+    ra, rb = 384.0, 640.0
     t[("kv", 4)] = ("x+", 256.0, (), 2.0)
     t[("tg", "b")] = ("x-", rb / 4, (), 3.0)
     t[("tg", "a")] = ("x-", ra / 4, (), 3.0)

time: 112 us -> 113 us (level)
  no operation moved by 1% of the time
where the time goes in v8:
time: 113 us; the launch traced here: 112 us
  Pallas kernels  108 us (96%)
  local copies, waits for them, and re-layouts  3.7 us (3%)
    pallas_call x1, Pallas kernels, on_device(): pl.pallas_call(kernel, out_shape=jax.ShapeDtypeStruct((CHUNK, 8192), bf),...  108 us
    unnamed x1, local copies, waits for them, and re-layouts  3.1 us

profile of v8, /device:TPU:15, one launch (start us, length us, event | category | flops | bytes accessed | tf_op | source)
XLA Modules:
  0.0 111.6 jit_solution(13776055684774930174)
XLA Ops:
  0.0 0.1 pad_maximum_fusion
  0.1 0.6 broadcast_in_dim.2.freq_ref
  0.7 107.8 %shard_map.73 = bf16[128,8192]{1,0:T(8,128)(2,1)} custom-call(bf16[512,1024]{1,0:T(8,128)(2,1)} %q_hbm.1, bf16[512,128]{1,0:T(8,128)(2,1)} %k_hbm.1, bf16[512,128]{1,0:T(8,128)(2,1)} %v_hbm.1, s32[3,512]{1,0:T(4,128)} %pos_hbm.1, s32[256,128]{1,0:T(8,128)} %bitcast.1, f32[8,128]{1,0:T(8,128)} %broadcast_in_dim.2.freq_ref, bf16[1024,128]{1,0:T(8,128)(2,1)} %w_hbm.1, ...), custom_call_target="tpu_custom_call" | custom-call | tf_op jit(solution)/shard_map/pallas_call | solution.py:592
  108.5 3.1 %copy.9 = bf16[128,8192]{1,0:T(8,128)(2,1)} copy(bf16[128,8192]{1,0:T(8,128)(2,1)} %shard_map.73) | data formatting | bytes 4194304
  (1 shorter events, 0.0 us)
